TPU v7x, 32 devices: a whole 2x2x4 slice. The times are simulated.
32 devices in a mesh: rows: 4 (over z), cols: 4 (over x, core), rep: 2 (over y).
Axes of the slice: x: 2, y: 2, z: 4, core: 2. Of those that a mesh axis runs over, the one named last changes fastest.
Arguments:
- matrix: float32 [16384, 8192], P(('rep', 'rows'), 'cols'), parts along dimension 0, may hold values from -0.0625 to 0.0625
- labels: int32 [16384], P(('rep', 'rows')), parts along dimension 0, may hold values from 0 to 1
- lambdas: float32 [64], P('rep'), parts along dimension 0, may hold values from 0.01 to 0.2
- x_prev: float32 [64, 8192], P('rep', 'cols'), parts along dimension 0, may hold values from -4 to 4
- w_prev: float32 [64, 8192], P('rep', 'cols'), parts along dimension 0, may hold values from -4 to 4
- p_prev: float32 [64, 8192], P('rep', 'cols'), parts along dimension 0, may hold values from -1.5 to 1.5
- z_prev: float32 [64, 8192], P('rep', 'rows'), parts along dimension 0, may hold values from -6 to 6
- u_prev: float32 [64, 8192], P('rep', 'rows'), parts along dimension 0, may hold values from -6 to 6
Outputs:
- coeffs: float32 [64, 8192], P('rep', 'cols'), parts along dimension 0
- sparse: float32 [64, 8192], P('rep', 'cols'), parts along dimension 0
- margins: float32 [64, 8192], P('rep', 'rows'), parts along dimension 0
- margin_dual: float32 [64, 8192], P('rep', 'rows'), parts along dimension 0
There are 2 independent parts, one for each index of `rep`. A program takes and returns all parts, laid end to end along the dimension named above; each array names one. Nothing has to cross between parts.
All inputs are finite; a program needn't handle non-finite values.
Results may differ from a plain program's by a relative error of at most 0.0003.
Values sent between devices are 32-bit elements; how exact they have to be, the bound alone decides.
No kernel may reach another device: no remote copies, remote signals or barrier semaphores. Data moves between devices by JAX's collectives and lax.ppermute only.
A program may use at most 128 MiB of HBM per device.

v0:
```python
import jax
import jax.numpy as jnp
from jax import lax
from jax.sharding import PartitionSpec as P

ITERS = 2
CG_STEPS = 5
NEWTON_STEPS = 8


HIGH = lax.Precision.HIGHEST


def apply_rows(vec, matrix):
    return lax.dot_general(
        vec, matrix, (((1,), (1,)), ((), ())), precision=HIGH, preferred_element_type=jnp.float32
    )


def apply_cols(vec, matrix):
    return lax.dot_general(
        vec, matrix, (((1,), (0,)), ((), ())), precision=HIGH, preferred_element_type=jnp.float32
    )


def proximal(target, sign):
    margin = target
    for step in range(NEWTON_STEPS):
        grad = margin - target - sign * jax.nn.sigmoid(-sign * margin)
        hess = 1.0 + jax.nn.sigmoid(margin) * jax.nn.sigmoid(-margin)
        margin = margin - grad / hess
    return margin


def forward(vec, matrix):
    return lax.psum(apply_rows(vec, matrix), "cols")


def forward_with_norm(vec, matrix):
    return lax.psum((apply_rows(vec, matrix), jnp.sum(vec * vec, axis=1)), "cols")


def backward(vec, matrix):
    partial_sum = apply_cols(vec, matrix)
    return lax.psum(partial_sum, "rows")


def squared_norm(value):
    return lax.psum(jnp.sum(value * value, axis=1), "cols")


def cg_image(direction, matrix):
    mapped, dd_part = forward_with_norm(direction, matrix)
    sq_part = jnp.sum(mapped * mapped, axis=1)
    back, sq_total = lax.psum((apply_cols(mapped, matrix), sq_part), "rows")
    curv_value = dd_part + sq_total
    return (direction + back, curv_value)


def local(matrix, labels, lambdas, x_prev, w_prev, p_prev, z_prev, u_prev):
    sign = (2.0 * labels.astype(jnp.float32) - 1.0)[None, :]
    coeffs, sparse, dual = (x_prev, w_prev, p_prev)
    margins, margin_dual = (z_prev, u_prev)
    for outer in range(ITERS):
        resid = (
            sparse
            - dual
            - coeffs
            + backward(margins - margin_dual - forward(coeffs, matrix), matrix)
        )
        direction = resid
        norm_now = squared_norm(resid)
        for step in range(CG_STEPS):
            image, curv_value = cg_image(direction, matrix)
            alpha = norm_now / curv_value
            coeffs = coeffs + alpha[:, None] * direction
            resid = resid - alpha[:, None] * image
            if step + 1 < CG_STEPS:
                norm_next = squared_norm(resid)
                direction = resid + (norm_next / norm_now)[:, None] * direction
                norm_now = norm_next
        target = forward(coeffs, matrix) + margin_dual
        margins = proximal(target, sign)
        margin_dual = target - margins
        total = coeffs + dual
        sparse = jnp.sign(total) * jnp.maximum(jnp.abs(total) - lambdas[:, None], 0.0)
        dual = total - sparse
    return (coeffs, sparse, margins, margin_dual)


def solution(mesh):
    return jax.shard_map(
        local,
        mesh=mesh,
        in_specs=(
            P(("rep", "rows"), "cols"),
            P(("rep", "rows")),
            P("rep"),
            P("rep", "cols"),
            P("rep", "cols"),
            P("rep", "cols"),
            P("rep", "rows"),
            P("rep", "rows"),
        ),
        out_specs=(P("rep", "cols"), P("rep", "cols"), P("rep", "rows"), P("rep", "rows")),
        check_vma=False,
    )
```

profile of v0, /device:TPU:0, one launch (start us, length us, event | category | flops | bytes accessed | tf_op | source)
XLA Modules:
  0.0 1297.5 jit_solution(16217579853619619662)
XLA Ops:
  7.3 19.3 %fusion.16 = f32[32,2048]{1,0:T(8,128)} fusion(f32[32,2048]{1,0:T(8,128)} %param.11, f32[2048,2048]{1,0:T(8,128)} %param.8), kind=kOutput, calls=%fused_computation.80 | convolution fusion | flops 1610612736 | bytes 17301504 | tf_op jit(solution)/shard_map/dot_general | solution.py:15
  26.6 35.1 %all-reduce.24.cloned.1.call-done = f32[32,2048]{1,0:T(8,128)} async-done(((f32[32,2048]{1,0:T(8,128)}), f32[32,2048]{1,0:T(8,128)}) %all-reduce.24.cloned.1.call-update) | async-done | bytes 262160 | tf_op jit(solution)/shard_map/psum | solution.py:36
  61.8 13.8 %fusion.4 = f32[32,2048]{1,0:T(8,128)} fusion(f32[2048,2048]{1,0:T(8,128)} %param.8, f32[32,2048]{1,0:T(8,128)} %all-reduce.24.cloned.1.call-done, f32[32,2048]{1,0:T(8,128)S(1)} %copy-done.14, f32[32,2048]{1,0:T(8,128)S(1)} %copy-done.3), kind=kOutput, calls=%fused_computation.57 | convolution fusion | flops 1610743808 | bytes 17825792 | tf_op jit(solution)/shard_map/dot_general | solution.py:21
  75.8 35.3 %all-reduce.26.cloned.1.call-done = f32[32,2048]{1,0:T(8,128)} async-done(((f32[32,2048]{1,0:T(8,128)}), f32[32,2048]{1,0:T(8,128)}) %all-reduce.26.cloned.1.call-update) | async-done | bytes 262160 | tf_op jit(solution)/shard_map/psum | solution.py:45
  112.3 19.2 %fusion.17 = f32[32,2048]{1,0:T(8,128)} fusion(f32[32,2048]{1,0:T(8,128)S(1)} %get-tuple-element.32, f32[2048,2048]{1,0:T(8,128)} %param.8), kind=kOutput, calls=%fused_computation.81 | convolution fusion | flops 1610612736 | bytes 17301504 | tf_op jit(solution)/shard_map/dot_general | solution.py:15
  137.2 26.6 %all-reduce.28.cloned.1.call-done = f32[32,2048]{1,0:T(8,128)} async-done(((f32[32,2048]{1,0:T(8,128)}), f32[32,2048]{1,0:T(8,128)}) %all-reduce.28.cloned.1.call-update) | async-done | bytes 262160 | tf_op jit(solution)/shard_map/psum | solution.py:40
  163.8 15.9 %fusion.18 = f32[32,2048]{1,0:T(8,128)} fusion(f32[32,2048]{1,0:T(8,128)} %all-reduce.28.cloned.1.call-done, f32[2048,2048]{1,0:T(8,128)} %param.8), kind=kOutput, calls=%fused_computation.82 | convolution fusion | flops 1610612736 | bytes 17301504 | tf_op jit(solution)/shard_map/dot_general | solution.py:21
  179.9 11.8 psum.370
  191.7 23.6 %all-reduce.30.cloned.1.call-done = f32[32,2048]{1,0:T(8,128)} async-done(((f32[32,2048]{1,0:T(8,128)}), f32[32,2048]{1,0:T(8,128)}) %all-reduce.30.cloned.1.call-update) | async-done | bytes 262160 | tf_op jit(solution)/shard_map/psum | solution.py:55
  222.6 19.9 %fusion.10 = f32[32,2048]{1,0:T(8,128)} fusion(f32[2048,2048]{1,0:T(8,128)} %param.8, f32[32,2048]{1,0:T(8,128)S(1)} %get-tuple-element.32, f32[32]{0:T(128)S(1)} %div.247, f32[32,2048]{1,0:T(8,128)} %all-reduce.30.cloned.1.call-done, f32[32]{0:T(128)S(1)} %add_divide_fusion.1), kind=kOutput, calls=%fused_computation.75 | convolution fusion | flops 1610940416 | bytes 17563904 | tf_op jit(solution)/shard_map/dot_general | solution.py:15
  242.8 6.6 psum.373
  249.4 25.7 %all-reduce.32.cloned.1.call-done = f32[32,2048]{1,0:T(8,128)} async-done(((f32[32,2048]{1,0:T(8,128)}), f32[32,2048]{1,0:T(8,128)}) %all-reduce.32.cloned.1.call-update) | async-done | bytes 262160 | tf_op jit(solution)/shard_map/psum | solution.py:40
  275.1 15.9 %fusion.19 = f32[32,2048]{1,0:T(8,128)} fusion(f32[32,2048]{1,0:T(8,128)} %all-reduce.32.cloned.1.call-done, f32[2048,2048]{1,0:T(8,128)} %param.8), kind=kOutput, calls=%fused_computation.83 | convolution fusion | flops 1610612736 | bytes 17301504 | tf_op jit(solution)/shard_map/dot_general | solution.py:21
  291.2 11.8 psum.375
  303.0 23.6 %all-reduce.34.cloned.1.call-done = f32[32,2048]{1,0:T(8,128)} async-done(((f32[32,2048]{1,0:T(8,128)}), f32[32,2048]{1,0:T(8,128)}) %all-reduce.34.cloned.1.call-update) | async-done | bytes 262160 | tf_op jit(solution)/shard_map/psum | solution.py:55
  333.9 19.2 %fusion.20 = f32[32,2048]{1,0:T(8,128)} fusion(f32[32,2048]{1,0:T(8,128)S(1)} %get-tuple-element.28, f32[2048,2048]{1,0:T(8,128)} %param.8), kind=kOutput, calls=%fused_computation.84 | convolution fusion | flops 1610612736 | bytes 17301504 | tf_op jit(solution)/shard_map/dot_general | solution.py:15
  353.1 6.6 psum.378
  359.7 25.9 %all-reduce.36.cloned.1.call-done = f32[32,2048]{1,0:T(8,128)} async-done(((f32[32,2048]{1,0:T(8,128)}), f32[32,2048]{1,0:T(8,128)}) %all-reduce.36.cloned.1.call-update) | async-done | bytes 262160 | tf_op jit(solution)/shard_map/psum | solution.py:40
  385.6 15.9 %fusion.21 = f32[32,2048]{1,0:T(8,128)} fusion(f32[32,2048]{1,0:T(8,128)} %all-reduce.36.cloned.1.call-done, f32[2048,2048]{1,0:T(8,128)} %param.8), kind=kOutput, calls=%fused_computation.85 | convolution fusion | flops 1610612736 | bytes 17301504 | tf_op jit(solution)/shard_map/dot_general | solution.py:21
  401.8 11.8 psum.380
  413.6 23.6 %all-reduce.38.cloned.1.call-done = f32[32,2048]{1,0:T(8,128)} async-done(((f32[32,2048]{1,0:T(8,128)}), f32[32,2048]{1,0:T(8,128)}) %all-reduce.38.cloned.1.call-update) | async-done | bytes 262160 | tf_op jit(solution)/shard_map/psum | solution.py:55
  444.4 19.2 %fusion.22 = f32[32,2048]{1,0:T(8,128)} fusion(f32[32,2048]{1,0:T(8,128)S(1)} %get-tuple-element.24, f32[2048,2048]{1,0:T(8,128)} %param.8), kind=kOutput, calls=%fused_computation.86 | convolution fusion | flops 1610612736 | bytes 17301504 | tf_op jit(solution)/shard_map/dot_general | solution.py:15
  463.7 6.6 psum.383
  470.3 25.9 %all-reduce.40.cloned.1.call-done = f32[32,2048]{1,0:T(8,128)} async-done(((f32[32,2048]{1,0:T(8,128)}), f32[32,2048]{1,0:T(8,128)}) %all-reduce.40.cloned.1.call-update) | async-done | bytes 262160 | tf_op jit(solution)/shard_map/psum | solution.py:40
  496.2 15.9 %fusion.23 = f32[32,2048]{1,0:T(8,128)} fusion(f32[32,2048]{1,0:T(8,128)} %all-reduce.40.cloned.1.call-done, f32[2048,2048]{1,0:T(8,128)} %param.8), kind=kOutput, calls=%fused_computation.87 | convolution fusion | flops 1610612736 | bytes 17301504 | tf_op jit(solution)/shard_map/dot_general | solution.py:21
  512.3 11.8 psum.385
  524.1 23.6 %all-reduce.42.cloned.1.call-done = f32[32,2048]{1,0:T(8,128)} async-done(((f32[32,2048]{1,0:T(8,128)}), f32[32,2048]{1,0:T(8,128)}) %all-reduce.42.cloned.1.call-update) | async-done | bytes 262160 | tf_op jit(solution)/shard_map/psum | solution.py:55
  554.8 20.0 %fusion.7 = f32[32,2048]{1,0:T(8,128)} fusion(f32[2048,2048]{1,0:T(8,128)} %param.8, f32[32,2048]{1,0:T(8,128)S(1)} %get-tuple-element.22, f32[32,2048]{1,0:T(8,128)S(1)} %get-tuple-element.24, f32[32]{0:T(128)S(1)} %div.253), kind=kOutput, calls=%fused_computation.61 | convolution fusion | flops 1610743808 | bytes 17563776 | tf_op jit(solution)/shard_map/dot_general | solution.py:15
  575.1 6.6 psum.388
  581.7 25.7 %all-reduce.44.cloned.1.call-done = f32[32,2048]{1,0:T(8,128)} async-done(((f32[32,2048]{1,0:T(8,128)}), f32[32,2048]{1,0:T(8,128)}) %all-reduce.44.cloned.1.call-update) | async-done | bytes 262160 | tf_op jit(solution)/shard_map/psum | solution.py:40
  608.4 12.2 psum.390
  620.9 19.2 %fusion.24 = f32[32,2048]{1,0:T(8,128)} fusion(f32[32,2048]{1,0:T(8,128)S(1)} %multiply_add_fusion.5, f32[2048,2048]{1,0:T(8,128)} %param.8), kind=kOutput, calls=%fused_computation.88 | convolution fusion | flops 1610612736 | bytes 17301504 | tf_op jit(solution)/shard_map/dot_general | solution.py:15
  640.3 29.4 %all-reduce.46.cloned.1.call-done = f32[32,2048]{1,0:T(8,128)} async-done(((f32[32,2048]{1,0:T(8,128)}), f32[32,2048]{1,0:T(8,128)}) %all-reduce.46.cloned.1.call-update) | async-done | bytes 262160 | tf_op jit(solution)/shard_map/psum | solution.py:36
  670.7 18.1 %fusion = f32[32,2048]{1,0:T(8,128)} fusion(f32[2048,2048]{1,0:T(8,128)} %param.8, f32[32,2048]{1,0:T(8,128)} %all-reduce.46.cloned.1.call-done, f32[32,2048]{1,0:T(8,128)S(1)} %add.444, f32[2048]{0:T(1024)S(1)} %get-tuple-element.34, f32[2048]{0:T(1024)S(1)} %get-tuple-element.33), kind=kOutput, calls=%fused_computation.26 | convolution fusion | flops 1619197952 | bytes 17580032 | tf_op jit(solution)/shard_map/dot_general | solution.py:21
  689.1 35.3 %all-reduce.48.cloned.1.call-done = f32[32,2048]{1,0:T(8,128)} async-done(((f32[32,2048]{1,0:T(8,128)}), f32[32,2048]{1,0:T(8,128)}) %all-reduce.48.cloned.1.call-update) | async-done | bytes 262160 | tf_op jit(solution)/shard_map/psum | solution.py:45
  725.7 19.2 %fusion.25 = f32[32,2048]{1,0:T(8,128)} fusion(f32[32,2048]{1,0:T(8,128)S(1)} %get-tuple-element.19, f32[2048,2048]{1,0:T(8,128)} %param.8), kind=kOutput, calls=%fused_computation.89 | convolution fusion | flops 1610612736 | bytes 17301504 | tf_op jit(solution)/shard_map/dot_general | solution.py:15
  750.6 26.6 %all-reduce.50.cloned.1.call-done = f32[32,2048]{1,0:T(8,128)} async-done(((f32[32,2048]{1,0:T(8,128)}), f32[32,2048]{1,0:T(8,128)}) %all-reduce.50.cloned.1.call-update) | async-done | bytes 262160 | tf_op jit(solution)/shard_map/psum | solution.py:40
  777.2 15.9 %fusion.26 = f32[32,2048]{1,0:T(8,128)} fusion(f32[32,2048]{1,0:T(8,128)} %all-reduce.50.cloned.1.call-done, f32[2048,2048]{1,0:T(8,128)} %param.8), kind=kOutput, calls=%fused_computation.90 | convolution fusion | flops 1610612736 | bytes 17301504 | tf_op jit(solution)/shard_map/dot_general | solution.py:21
  793.3 11.8 psum.395
  805.1 23.6 %all-reduce.52.cloned.1.call-done = f32[32,2048]{1,0:T(8,128)} async-done(((f32[32,2048]{1,0:T(8,128)}), f32[32,2048]{1,0:T(8,128)}) %all-reduce.52.cloned.1.call-update) | async-done | bytes 262160 | tf_op jit(solution)/shard_map/psum | solution.py:55
  836.0 19.9 %fusion.11 = f32[32,2048]{1,0:T(8,128)} fusion(f32[2048,2048]{1,0:T(8,128)} %param.8, f32[32,2048]{1,0:T(8,128)S(1)} %get-tuple-element.19, f32[32]{0:T(128)S(1)} %div.288, f32[32,2048]{1,0:T(8,128)} %all-reduce.52.cloned.1.call-done, f32[32]{0:T(128)S(1)} %add_divide_fusion), kind=kOutput, calls=%fused_computation.76 | convolution fusion | flops 1610940416 | bytes 17563904 | tf_op jit(solution)/shard_map/dot_general | solution.py:15
  856.2 6.6 psum.398
  862.8 25.7 %all-reduce.54.cloned.1.call-done = f32[32,2048]{1,0:T(8,128)} async-done(((f32[32,2048]{1,0:T(8,128)}), f32[32,2048]{1,0:T(8,128)}) %all-reduce.54.cloned.1.call-update) | async-done | bytes 262160 | tf_op jit(solution)/shard_map/psum | solution.py:40
  888.5 15.9 %fusion.27 = f32[32,2048]{1,0:T(8,128)} fusion(f32[32,2048]{1,0:T(8,128)} %all-reduce.54.cloned.1.call-done, f32[2048,2048]{1,0:T(8,128)} %param.8), kind=kOutput, calls=%fused_computation.91 | convolution fusion | flops 1610612736 | bytes 17301504 | tf_op jit(solution)/shard_map/dot_general | solution.py:21
  904.6 11.8 psum.400
  916.4 23.6 %all-reduce.56.cloned.1.call-done = f32[32,2048]{1,0:T(8,128)} async-done(((f32[32,2048]{1,0:T(8,128)}), f32[32,2048]{1,0:T(8,128)}) %all-reduce.56.cloned.1.call-update) | async-done | bytes 262160 | tf_op jit(solution)/shard_map/psum | solution.py:55
  947.3 19.2 %fusion.28 = f32[32,2048]{1,0:T(8,128)} fusion(f32[32,2048]{1,0:T(8,128)S(1)} %get-tuple-element.15, f32[2048,2048]{1,0:T(8,128)} %param.8), kind=kOutput, calls=%fused_computation.92 | convolution fusion | flops 1610612736 | bytes 17301504 | tf_op jit(solution)/shard_map/dot_general | solution.py:15
  966.5 6.6 psum.403
  973.1 25.9 %all-reduce.58.cloned.1.call-done = f32[32,2048]{1,0:T(8,128)} async-done(((f32[32,2048]{1,0:T(8,128)}), f32[32,2048]{1,0:T(8,128)}) %all-reduce.58.cloned.1.call-update) | async-done | bytes 262160 | tf_op jit(solution)/shard_map/psum | solution.py:40
  999.0 15.9 %fusion.29 = f32[32,2048]{1,0:T(8,128)} fusion(f32[32,2048]{1,0:T(8,128)} %all-reduce.58.cloned.1.call-done, f32[2048,2048]{1,0:T(8,128)} %param.8), kind=kOutput, calls=%fused_computation.93 | convolution fusion | flops 1610612736 | bytes 17301504 | tf_op jit(solution)/shard_map/dot_general | solution.py:21
  1015.2 11.8 psum.405
  1027.0 23.6 %all-reduce.60.cloned.1.call-done = f32[32,2048]{1,0:T(8,128)} async-done(((f32[32,2048]{1,0:T(8,128)}), f32[32,2048]{1,0:T(8,128)}) %all-reduce.60.cloned.1.call-update) | async-done | bytes 262160 | tf_op jit(solution)/shard_map/psum | solution.py:55
  1057.8 19.2 %fusion.30 = f32[32,2048]{1,0:T(8,128)} fusion(f32[32,2048]{1,0:T(8,128)S(1)} %get-tuple-element.11, f32[2048,2048]{1,0:T(8,128)} %param.8), kind=kOutput, calls=%fused_computation.94 | convolution fusion | flops 1610612736 | bytes 17301504 | tf_op jit(solution)/shard_map/dot_general | solution.py:15
  1077.1 6.6 psum.408
  1083.7 25.9 %all-reduce.62.cloned.1.call-done = f32[32,2048]{1,0:T(8,128)} async-done(((f32[32,2048]{1,0:T(8,128)}), f32[32,2048]{1,0:T(8,128)}) %all-reduce.62.cloned.1.call-update) | async-done | bytes 262160 | tf_op jit(solution)/shard_map/psum | solution.py:40
  1109.6 15.9 %fusion.31 = f32[32,2048]{1,0:T(8,128)} fusion(f32[32,2048]{1,0:T(8,128)} %all-reduce.62.cloned.1.call-done, f32[2048,2048]{1,0:T(8,128)} %param.8), kind=kOutput, calls=%fused_computation.95 | convolution fusion | flops 1610612736 | bytes 17301504 | tf_op jit(solution)/shard_map/dot_general | solution.py:21
  1125.7 11.8 psum.410
  1137.5 23.8 %all-reduce.64.cloned.1.call-done = f32[32,2048]{1,0:T(8,128)} async-done(((f32[32,2048]{1,0:T(8,128)}), f32[32,2048]{1,0:T(8,128)}) %all-reduce.64.cloned.1.call-update) | async-done | bytes 262160 | tf_op jit(solution)/shard_map/psum | solution.py:55
  1168.4 20.0 %fusion.8 = f32[32,2048]{1,0:T(8,128)} fusion(f32[2048,2048]{1,0:T(8,128)} %param.8, f32[32,2048]{1,0:T(8,128)S(1)} %get-tuple-element.9, f32[32,2048]{1,0:T(8,128)S(1)} %get-tuple-element.11, f32[32]{0:T(128)S(1)} %div.294), kind=kOutput, calls=%fused_computation.62 | convolution fusion | flops 1610743808 | bytes 17563776 | tf_op jit(solution)/shard_map/dot_general | solution.py:15
  1188.6 6.6 psum.413
  1195.2 25.7 %all-reduce.66.cloned.1.call-done = f32[32,2048]{1,0:T(8,128)} async-done(((f32[32,2048]{1,0:T(8,128)}), f32[32,2048]{1,0:T(8,128)}) %all-reduce.66.cloned.1.call-update) | async-done | bytes 262160 | tf_op jit(solution)/shard_map/psum | solution.py:40
  1222.0 12.0 psum.415
  1235.1 19.3 %fusion.32 = f32[32,2048]{1,0:T(8,128)} fusion(f32[32,2048]{1,0:T(8,128)S(1)} %get-tuple-element.7, f32[2048,2048]{1,0:T(8,128)} %param.8), kind=kOutput, calls=%fused_computation.96 | convolution fusion | flops 1610612736 | bytes 17301504 | tf_op jit(solution)/shard_map/dot_general | solution.py:15
  1254.4 29.7 %all-reduce.68.cloned.1.call-done = f32[32,2048]{1,0:T(8,128)} async-done(((f32[32,2048]{1,0:T(8,128)}), f32[32,2048]{1,0:T(8,128)}) %all-reduce.68.cloned.1.call-update) | async-done | bytes 262160 | tf_op jit(solution)/shard_map/psum | solution.py:36
  (143 shorter events, 86.5 us)
Async XLA Ops:
  7.2 104.0 %copy-start.2 = (f32[32,2048]{1,0:T(8,128)S(1)}, f32[32,2048]{1,0:T(8,128)}, u32[]{:S(2)}) copy-start(f32[32,2048]{1,0:T(8,128)} %param.11) | copy-start | bytes 786436
  7.2 54.6 %copy-start.14 = (f32[32,2048]{1,0:T(8,128)S(1)}, f32[32,2048]{1,0:T(8,128)}, u32[]{:S(2)}) copy-start(f32[32,2048]{1,0:T(8,128)} %param.14) | copy-start | bytes 786436
  7.2 54.6 %copy-start.3 = (f32[32,2048]{1,0:T(8,128)S(1)}, f32[32,2048]{1,0:T(8,128)}, u32[]{:S(2)}) copy-start(f32[32,2048]{1,0:T(8,128)} %param.15) | copy-start | bytes 786436
  7.2 104.0 %copy-start.15 = (f32[32,2048]{1,0:T(8,128)S(1)}, f32[32,2048]{1,0:T(8,128)}, u32[]{:S(2)}) copy-start(f32[32,2048]{1,0:T(8,128)} %param.12) | copy-start | bytes 786436
  7.2 103.9 %copy-start.13 = (f32[32,2048]{1,0:T(8,128)S(1)}, f32[32,2048]{1,0:T(8,128)}, u32[]{:S(2)}) copy-start(f32[32,2048]{1,0:T(8,128)} %param.13) | copy-start | bytes 786436
  7.2 54.6 %all-reduce.24.cloned.1.call-start = ((), (), s32[]{:S(2)}) async-start(), calls=%async_computation | async-start | bytes 524288 | tf_op jit(solution)/shard_map/psum | solution.py:36
  26.6 84.5 %all-reduce.26.cloned.1.call-start = ((), (), s32[]{:S(2)}) async-start(), calls=%async_computation.1 | async-start | bytes 524288 | tf_op jit(solution)/shard_map/psum | solution.py:45
  75.6 88.2 %all-reduce.28.cloned.1.call-start = ((), (), s32[]{:S(2)}) async-start(), calls=%async_computation.2 | async-start | bytes 524288 | tf_op jit(solution)/shard_map/psum | solution.py:40
  131.5 83.8 %all-reduce.30.cloned.1.call-start = ((), (), s32[]{:S(2)}) async-start(), calls=%async_computation.3 | async-start | bytes 524288 | tf_op jit(solution)/shard_map/psum | solution.py:55
  163.8 16.0 %copy-start.5 = (f32[32,2048]{1,0:T(8,128)S(1)}, f32[32,2048]{1,0:T(8,128)}, u32[]{:S(2)}) copy-start(f32[32,2048]{1,0:T(8,128)} %all-reduce.28.cloned.1.call-done) | copy-start | bytes 786436
  179.7 95.4 %all-reduce.32.cloned.1.call-start = ((), (), s32[]{:S(2)}) async-start(), calls=%async_computation.4 | async-start | bytes 524288 | tf_op jit(solution)/shard_map/psum | solution.py:40
  215.3 27.3 %copy-start.1 = (f32[32,2048]{1,0:T(8,128)S(1)}, f32[32,2048]{1,0:T(8,128)}, u32[]{:S(2)}) copy-start(f32[32,2048]{1,0:T(8,128)} %all-reduce.30.cloned.1.call-done) | copy-start | bytes 786436
  242.5 84.1 %all-reduce.34.cloned.1.call-start = ((), (), s32[]{:S(2)}) async-start(), calls=%async_computation.5 | async-start | bytes 524288 | tf_op jit(solution)/shard_map/psum | solution.py:55
  275.1 16.0 %copy-start.6 = (f32[32,2048]{1,0:T(8,128)S(1)}, f32[32,2048]{1,0:T(8,128)}, u32[]{:S(2)}) copy-start(f32[32,2048]{1,0:T(8,128)} %all-reduce.32.cloned.1.call-done) | copy-start | bytes 786436
  291.0 94.6 %all-reduce.36.cloned.1.call-start = ((), (), s32[]{:S(2)}) async-start(), calls=%async_computation.6 | async-start | bytes 524288 | tf_op jit(solution)/shard_map/psum | solution.py:40
  353.1 84.1 %all-reduce.38.cloned.1.call-start = ((), (), s32[]{:S(2)}) async-start(), calls=%async_computation.7 | async-start | bytes 524288 | tf_op jit(solution)/shard_map/psum | solution.py:55
  385.6 16.0 %copy-start.7 = (f32[32,2048]{1,0:T(8,128)S(1)}, f32[32,2048]{1,0:T(8,128)}, u32[]{:S(2)}) copy-start(f32[32,2048]{1,0:T(8,128)} %all-reduce.36.cloned.1.call-done) | copy-start | bytes 786436
  401.6 94.6 %all-reduce.40.cloned.1.call-start = ((), (), s32[]{:S(2)}) async-start(), calls=%async_computation.8 | async-start | bytes 524288 | tf_op jit(solution)/shard_map/psum | solution.py:40
  463.6 84.1 %all-reduce.42.cloned.1.call-start = ((), (), s32[]{:S(2)}) async-start(), calls=%async_computation.9 | async-start | bytes 524288 | tf_op jit(solution)/shard_map/psum | solution.py:55
  496.2 16.0 %copy-start.8 = (f32[32,2048]{1,0:T(8,128)S(1)}, f32[32,2048]{1,0:T(8,128)}, u32[]{:S(2)}) copy-start(f32[32,2048]{1,0:T(8,128)} %all-reduce.40.cloned.1.call-done) | copy-start | bytes 786436
  512.1 95.2 %all-reduce.44.cloned.1.call-start = ((), (), s32[]{:S(2)}) async-start(), calls=%async_computation.10 | async-start | bytes 524288 | tf_op jit(solution)/shard_map/psum | solution.py:40
  554.8 85.5 %copy-start.16 = (s32[2048]{0:T(1024)S(1)}, s32[2048]{0:T(1024)}, u32[]{:S(2)}) copy-start(s32[2048]{0:T(1024)} %param.9) | copy-start | bytes 24580
  574.8 94.9 %all-reduce.46.cloned.1.call-start = ((), (), s32[]{:S(2)}) async-start(), calls=%async_computation.11 | async-start | bytes 524288 | tf_op jit(solution)/shard_map/psum | solution.py:36
  640.1 84.4 %all-reduce.48.cloned.1.call-start = ((), (), s32[]{:S(2)}) async-start(), calls=%async_computation.12 | async-start | bytes 524288 | tf_op jit(solution)/shard_map/psum | solution.py:45
  670.7 53.7 %copy-start.17 = (f32[32]{0:T(128)S(1)}, f32[32]{0:T(128)}, u32[]{:S(2)}) copy-start(f32[32]{0:T(128)} %param.10) | copy-start | bytes 388
  688.9 88.3 %all-reduce.50.cloned.1.call-start = ((), (), s32[]{:S(2)}) async-start(), calls=%async_computation.13 | async-start | bytes 524288 | tf_op jit(solution)/shard_map/psum | solution.py:40
  744.9 83.8 %all-reduce.52.cloned.1.call-start = ((), (), s32[]{:S(2)}) async-start(), calls=%async_computation.14 | async-start | bytes 524288 | tf_op jit(solution)/shard_map/psum | solution.py:55
  777.2 16.0 %copy-start.12 = (f32[32,2048]{1,0:T(8,128)S(1)}, f32[32,2048]{1,0:T(8,128)}, u32[]{:S(2)}) copy-start(f32[32,2048]{1,0:T(8,128)} %all-reduce.50.cloned.1.call-done) | copy-start | bytes 786436
  793.1 95.4 %all-reduce.54.cloned.1.call-start = ((), (), s32[]{:S(2)}) async-start(), calls=%async_computation.15 | async-start | bytes 524288 | tf_op jit(solution)/shard_map/psum | solution.py:40
  828.7 27.3 %copy-start = (f32[32,2048]{1,0:T(8,128)S(1)}, f32[32,2048]{1,0:T(8,128)}, u32[]{:S(2)}) copy-start(f32[32,2048]{1,0:T(8,128)} %all-reduce.52.cloned.1.call-done) | copy-start | bytes 786436
  855.9 84.1 %all-reduce.56.cloned.1.call-start = ((), (), s32[]{:S(2)}) async-start(), calls=%async_computation.16 | async-start | bytes 524288 | tf_op jit(solution)/shard_map/psum | solution.py:55
  888.5 16.0 %copy-start.9 = (f32[32,2048]{1,0:T(8,128)S(1)}, f32[32,2048]{1,0:T(8,128)}, u32[]{:S(2)}) copy-start(f32[32,2048]{1,0:T(8,128)} %all-reduce.54.cloned.1.call-done) | copy-start | bytes 786436
  904.4 94.6 %all-reduce.58.cloned.1.call-start = ((), (), s32[]{:S(2)}) async-start(), calls=%async_computation.17 | async-start | bytes 524288 | tf_op jit(solution)/shard_map/psum | solution.py:40
  966.5 84.1 %all-reduce.60.cloned.1.call-start = ((), (), s32[]{:S(2)}) async-start(), calls=%async_computation.18 | async-start | bytes 524288 | tf_op jit(solution)/shard_map/psum | solution.py:55
  999.0 16.0 %copy-start.10 = (f32[32,2048]{1,0:T(8,128)S(1)}, f32[32,2048]{1,0:T(8,128)}, u32[]{:S(2)}) copy-start(f32[32,2048]{1,0:T(8,128)} %all-reduce.58.cloned.1.call-done) | copy-start | bytes 786436
  1015.0 94.6 %all-reduce.62.cloned.1.call-start = ((), (), s32[]{:S(2)}) async-start(), calls=%async_computation.19 | async-start | bytes 524288 | tf_op jit(solution)/shard_map/psum | solution.py:40
  1077.0 84.2 %all-reduce.64.cloned.1.call-start = ((), (), s32[]{:S(2)}) async-start(), calls=%async_computation.20 | async-start | bytes 524288 | tf_op jit(solution)/shard_map/psum | solution.py:55
  1109.6 16.0 %copy-start.11 = (f32[32,2048]{1,0:T(8,128)S(1)}, f32[32,2048]{1,0:T(8,128)}, u32[]{:S(2)}) copy-start(f32[32,2048]{1,0:T(8,128)} %all-reduce.62.cloned.1.call-done) | copy-start | bytes 786436
  1125.5 95.4 %all-reduce.66.cloned.1.call-start = ((), (), s32[]{:S(2)}) async-start(), calls=%async_computation.21 | async-start | bytes 524288 | tf_op jit(solution)/shard_map/psum | solution.py:40
  1188.3 95.8 %all-reduce.68.cloned.1.call-start = ((), (), s32[]{:S(2)}) async-start(), calls=%async_computation.22 | async-start | bytes 524288 | tf_op jit(solution)/shard_map/psum | solution.py:36
  1235.1 55.3 %copy-start.4 = (f32[32,2048]{1,0:T(8,128)}, f32[32,2048]{1,0:T(8,128)S(1)}, u32[]{:S(2)}) copy-start(f32[32,2048]{1,0:T(8,128)S(1)} %get-tuple-element.7) | copy-start | bytes 786436
Sparse Core Ops, SparseCore 0:
  26.7 35.0 all-reduce.23
  75.7 35.3 all-reduce.25
  131.6 32.1 all-reduce.27
  179.8 35.3 all-reduce.29
  242.6 32.4 all-reduce.31
  291.1 35.3 all-reduce.33
  353.2 32.3 all-reduce.35
  401.7 35.3 all-reduce.37
  463.8 32.3 all-reduce.39
  512.3 35.4 all-reduce.41
  574.9 32.4 all-reduce.43
  640.2 29.4 all-reduce.45
  689.0 35.3 all-reduce.47
  745.0 32.1 all-reduce.49
  793.2 35.3 all-reduce.51
  856.0 32.4 all-reduce.53
  904.5 35.3 all-reduce.55
  966.6 32.3 all-reduce.57
  1015.1 35.3 all-reduce.59
  1077.2 32.3 all-reduce.61
  1125.7 35.5 all-reduce.63
  1188.5 32.4 all-reduce.65
  1254.6 29.4 all-reduce.67
where the time goes:
time: 1310 us; the launch traced here: 1300 us
  waiting for transfers between devices  614 us (47%)
  matrix products  412 us (31%)
  blocking collectives  230 us (18%)
  other arithmetic  25.7 us (2%)
  between operations  14.8 us (1%)
    psum x10, waiting for transfers between devices, forward_with_norm(): lax.psum((apply_rows(vec, matrix), jnp.sum(vec * vec, axis=1)), 'cols')  260 us
    dot_general x13, matrix products, apply_rows(): lax.dot_general(vec, matrix, (((1,), (1,)), ((), ())), precision=HIGH, pr...  253 us
    psum x8, waiting for transfers between devices, cg_image(): back, sq_total = lax.psum((apply_cols(mapped, matrix), sq_part), 'rows')  189 us
    dot_general x10, matrix products, apply_cols(): lax.dot_general(vec, matrix, (((1,), (0,)), ((), ())), precision=HIGH, pr...  159 us
    psum x10, blocking collectives, cg_image(): back, sq_total = lax.psum((apply_cols(mapped, matrix), sq_part), 'rows')  118 us
    psum x3, waiting for transfers between devices, forward(): return lax.psum(apply_rows(vec, matrix), 'cols')  94.2 us
    psum x2, waiting for transfers between devices, backward(): return lax.psum(partial_sum, 'rows')  70.6 us
    psum x10, blocking collectives, squared_norm(): return lax.psum(jnp.sum(value * value, axis=1), 'cols')  58.7 us
  transfers between devices with their start and end apart: 23, of which 23 were waited for; matrix products, arithmetic and copies ran while one was open for 0% of the time, Pallas kernels for 0%

commit v1 on v0

v1 whole, which is shorter than its diff:
```python
import functools

import jax
import jax.numpy as jnp
from jax import lax
from jax.experimental import pallas as pl
from jax.experimental.pallas import tpu as pltpu
from jax.sharding import PartitionSpec as P

ITERS = 2
CG_STEPS = 5
NEWTON_STEPS = 8
LANES = 128
SUBLANES = 8
ROW_TILE = 256
COL_TILE = 512
KERNEL_VMEM = 6 * 2**20
PREP_VMEM = 10 * 2**20


f32 = jnp.float32
bf16 = jnp.bfloat16
VM = pl.BlockSpec(memory_space=pltpu.VMEM)


def call(body, outs, args, weights=0, flops=0):
    args = list(args)
    for i in range(len(args) - weights, len(args)):
        args[i] = pltpu.with_memory_space_constraint(args[i], pltpu.VMEM)
    moved = sum(a.size * a.dtype.itemsize for a in args)
    return pl.pallas_call(
        body,
        in_specs=[VM] * len(args),
        out_specs=[VM] * len(outs),
        out_shape=[jax.ShapeDtypeStruct(s, f32) for s in outs],
        compiler_params=pltpu.CompilerParams(vmem_limit_bytes=KERNEL_VMEM),
        cost_estimate=pl.CostEstimate(flops=flops, bytes_accessed=moved, transcendentals=0),
    )(*args)


def parts_of(x):
    hi = x.astype(bf16)
    return hi, (x - hi.astype(f32)).astype(bf16)


def stacked(x):
    return jnp.concatenate(parts_of(x), 0)


def product(lhs, hi, lo, rows, cols):
    acc = jnp.dot(lhs, hi[rows, cols], preferred_element_type=f32)
    return acc + jnp.dot(lhs, lo[rows, cols], preferred_element_type=f32)


def folded(acc):
    m = acc.shape[0] // 2
    return acc[:m] + acc[m:]


def span(j, n):
    return pl.ds(pl.multiple_of(j * n, n), n)


def row_sum(x):
    return jnp.sum(x, axis=1, keepdims=True)


def wide(x):
    return jnp.broadcast_to(x, (x.shape[0], LANES))


def put_blocks(ref, value, at=0):
    m = value.shape[0]
    for j in range(value.shape[1] // LANES):
        ref[at + j * m : at + (j + 1) * m, :] = value[:, j * LANES : (j + 1) * LANES]


def get_blocks(value, m, n):
    return jnp.concatenate([value[j * m : (j + 1) * m, :] for j in range(n // LANES)], 1)


def pack(columns):
    groups = columns[0].shape[0] // SUBLANES
    width = LANES // (groups * len(columns))
    slot = lax.broadcasted_iota(jnp.int32, (SUBLANES, LANES), 1) // width
    tile = jnp.zeros((SUBLANES, LANES), f32)
    for i, c in enumerate(columns):
        for a in range(groups):
            part = wide(c[a * SUBLANES : (a + 1) * SUBLANES])
            tile = jnp.where(slot == i * groups + a, part, tile)
    return tile


def unpack(tile, paths, i, n):
    groups = paths // SUBLANES
    width = LANES // (groups * n)
    at = [(i * groups + a) * width for a in range(groups)]
    return jnp.concatenate([tile[:, c : c + 1] for c in at], 0)


def tree(items):
    if len(items) == 1:
        return items[0]
    h = len(items) // 2
    return tree(items[:h]) + tree(items[h:])


def send_order(rows_n):
    return [k for k in (*range(rows_n // 2, rows_n), *range(1, rows_n // 2)) if k > 0]


def xor_perm(x, axis, size, k):
    return lax.ppermute(x, axis, [(i, i ^ k) for i in range(size)])


def prep_kernel(m_ref, x_ref, hi, lo, t_hi, t_lo, u_ref):
    tile = m_ref.shape[0]
    paths = x_ref.shape[0]
    step = pl.program_id(0)
    rows = span(step, tile)
    h, l = parts_of(m_ref[...])
    hi[rows, :] = h
    lo[rows, :] = l
    ht, lt = h.T, l.T
    t_hi[:, rows] = ht
    t_lo[:, rows] = lt
    lhs = stacked(x_ref[...])
    acc = jnp.dot(lhs, ht, preferred_element_type=f32)
    u = folded(acc + jnp.dot(lhs, lt, preferred_element_type=f32))
    blocks = tile // LANES
    core = lax.rem(lax.axis_index("cols"), 2)
    per_half = pl.num_programs(0) // 2
    place = lax.rem(step + core * per_half, 2 * per_half)
    for j in range(blocks):
        u_ref[span(place * blocks + j, paths), :] = u[:, j * LANES : (j + 1) * LANES]


def prep(matrix, x):
    n, k = matrix.shape
    tile = min(ROW_TILE, n // 2)
    paths = x.shape[0]
    return pl.pallas_call(
        prep_kernel,
        grid=(n // tile,),
        in_specs=[pl.BlockSpec((tile, k), lambda i: (i, 0)), VM],
        out_specs=[VM] * 5,
        out_shape=[
            pltpu.VMEM((n, k), bf16),
            pltpu.VMEM((n, k), bf16),
            pltpu.VMEM((k, n), bf16),
            pltpu.VMEM((k, n), bf16),
            jax.ShapeDtypeStruct((paths * n // LANES, LANES), f32),
        ],
        name="prep",
        compiler_params=pltpu.CompilerParams(vmem_limit_bytes=PREP_VMEM),
    )(matrix, x)


def prox(target, sign):
    m = target
    for _ in range(NEWTON_STEPS):
        e = jnp.exp(-jnp.abs(m))
        big = 1.0 / (1.0 + e)
        small = e * big
        pull = jnp.where((m >= 0.0) == (sign > 0.0), small, big)
        m = m - (m - target - sign * pull) / (1.0 + big * small)
    return m


def local(rows_n, cols_n, matrix, labels, lambdas, x_prev, w_prev, p_prev, z_prev, u_prev):
    paths, nf = x_prev.shape
    ns = z_prev.shape[1]
    fc = nf // rows_n
    half = ns // 2
    tile = min(COL_TILE, half)
    work = 2 * 4 * paths * nf * ns
    full_f, full_s, chunk, one = (paths, nf), (paths, ns), (paths, fc), (paths, LANES)
    scal = (SUBLANES, LANES)
    top = paths * fc // LANES
    mid = paths * half // LANES
    piece = (top + SUBLANES, LANES)
    split = (mid + SUBLANES, LANES)
    order = send_order(rows_n)
    early, late = list(range(max(rows_n // 2, 1))), list(range(max(rows_n // 2, 1), rows_n))
    ahead, behind = order[:2], order[2:] + [0]

    def send_rows(values):
        got = {}
        for k in order:
            got[k] = xor_perm(values[k], "rows", rows_n, k)
        return got

    def sum_cols(other, own):
        s = own + xor_perm(other, "cols", cols_n, 1)
        k = 2
        while k < cols_n:
            s = s + xor_perm(s, "cols", cols_n, k)
            k *= 2
        return s, xor_perm(s, "cols", cols_n, 1)

    def core_half():
        return lax.rem(lax.axis_index("cols"), 2)

    def fwd_early_kernel(*refs):
        got, (th, tl, acc_ref) = refs[:-3], refs[-3:]
        me = lax.axis_index("rows")
        lhs = [stacked(g[...]) for g in got]

        @pl.loop(0, ns // tile)
        def _(j):
            cols = span(j, tile)
            acc = [product(v, th, tl, span(me ^ k, fc), cols) for v, k in zip(lhs, early)]
            acc_ref[:, cols] = folded(sum(acc[1:], acc[0]))

    def fwd_half(h, got, acc_ref, th, tl, out_ref):
        me = lax.axis_index("rows")
        lhs = [stacked(g[...]) for g in got]

        @pl.loop(0, half // tile)
        def _(j):
            cols = pl.ds(pl.multiple_of(h * half + j * tile, tile), tile)
            u = acc_ref[:, cols]
            acc = [product(v, th, tl, span(me ^ k, fc), cols) for v, k in zip(lhs, late)]
            if acc:
                u = u + folded(sum(acc[1:], acc[0]))
            for i in range(tile // LANES):
                rows = span(j * (tile // LANES) + i, paths)
                out_ref[rows, :] = u[:, i * LANES : (i + 1) * LANES]

    def fwd_other_kernel(first, *refs):
        got, refs = refs[:rows_n], refs[rows_n:]
        if not first:
            d_old, refs = refs[0], refs[1:]
        acc_ref, th, tl, out_ref, r_ref, scal_ref = refs
        me = lax.axis_index("rows")
        for g, k in zip(got, early + late):
            r_ref[:, span(me ^ k, fc)] = g[...]
        r = r_ref[...]
        rr = row_sum(r * r)
        rd = jnp.zeros_like(rr) if first else row_sum(r * d_old[...])
        scalars = pack([rr, rd])
        scal_ref[...] = scalars
        out_ref[mid:, :] = scalars
        fwd_half(1 - core_half(), got[len(early) :], acc_ref, th, tl, out_ref)

    def fwd_own_kernel(*refs):
        got, (scal_ref, acc_ref, th, tl, out_ref) = refs[:-5], refs[-5:]
        out_ref[mid:, :] = scal_ref[...]
        fwd_half(core_half(), got, acc_ref, th, tl, out_ref)

    def bwd_own_kernel(first, *refs):
        if first:
            own, r_ref, h_ref, l_ref, ad_ref, d_ref, rr_ref, dd_ref, acc_ref = refs
        else:
            own, r_ref, ad_old, d_old, rr_old, dd_old = refs[:6]
            h_ref, l_ref, ad_ref, d_ref, rr_ref, dd_ref, acc_ref = refs[6:]
        me, core = lax.axis_index("rows"), core_half()
        rr = unpack(own[mid:, :], paths, 0, 2)
        ad = get_blocks(own[...], paths, half)
        if first:
            dd = rr
            d_ref[...] = r_ref[...]
        else:
            rd = unpack(own[mid:, :], paths, 1, 2)
            beta = rr / rr_old[:, :1]
            dd = rr + 2.0 * beta * rd + beta * beta * dd_old[:, :1]
            d_ref[...] = r_ref[...] + beta * d_old[...]
            ad = ad + beta * ad_old[:, span(core, half)]
        ad_ref[...] = ad
        rr_ref[...] = wide(rr)
        dd_ref[...] = wide(dd)
        if acc_ref is None:
            return
        lhs = stacked(ad)

        @pl.loop(0, rows_n)
        def _(k):
            acc = product(lhs, h_ref, l_ref, span(core, half), span(me ^ k, fc))
            acc_ref[:, span(k, fc)] = folded(acc)

    def join_ad(first, got, own_ref, rr_ref, ad_old, rr_old, ad_ref):
        core = core_half()
        ad = get_blocks(got[...], paths, half)
        if not first:
            ad = ad + (rr_ref[:, :1] / rr_old[:, :1]) * ad_old[:, span(1 - core, half)]
        ad_ref[:, span(core, half)] = own_ref[...]
        ad_ref[:, span(1 - core, half)] = ad
        return ad

    def write_piece(ref, value, scalars):
        put_blocks(ref, value)
        ref[top:, :] = scalars

    def bwd_other(ks, ad, scalars, acc_ref, h_ref, l_ref, outs):
        me, core = lax.axis_index("rows"), core_half()
        lhs = stacked(ad)
        for k, ref in zip(ks, outs):
            acc = product(lhs, h_ref, l_ref, span(1 - core, half), span(me ^ k, fc))
            write_piece(ref, acc_ref[:, k * fc : (k + 1) * fc] + folded(acc), scalars)

    def bwd_ahead_kernel(first, *refs):
        got, own_ref, rr_ref = refs[:3]
        ad_old = rr_old = None
        refs = refs[3:]
        if not first:
            ad_old, rr_old = refs[:2]
            refs = refs[2:]
        acc_ref, h_ref, l_ref, ad_ref, scal_ref = refs[:5]
        ad = join_ad(first, got, own_ref, rr_ref, ad_old, rr_old, ad_ref)
        own = own_ref[...]
        scalars = pack([row_sum(own * own) + row_sum(ad * ad)])
        scal_ref[...] = scalars
        bwd_other(ahead, ad, scalars, acc_ref, h_ref, l_ref, refs[5:])

    def bwd_behind_kernel(ad_ref, scal_ref, acc_ref, h_ref, l_ref, *outs):
        ad = ad_ref[:, span(1 - core_half(), half)]
        bwd_other(behind, ad, scal_ref[...], acc_ref, h_ref, l_ref, outs)

    def last_kernel(got, own_ref, rr_ref, ad_old, rr_old, ad_ref, scal_ref):
        ad = join_ad(False, got, own_ref, rr_ref, ad_old, rr_old, ad_ref)
        own = own_ref[...]
        scal_ref[...] = pack([row_sum(own * own) + row_sum(ad * ad)])

    def whole_pieces(ks, v, h_ref, l_ref, outs):
        me = lax.axis_index("rows")
        lhs = stacked(v)
        for k, ref in zip(ks, outs):
            acc = product(lhs, h_ref, l_ref, slice(None), span(me ^ k, fc))
            write_piece(ref, folded(acc), jnp.zeros(scal, f32))

    def whole_behind_kernel(v_ref, h_ref, l_ref, *outs):
        whole_pieces(behind, v_ref[...], h_ref, l_ref, outs)

    def alpha_of(rr_ref, dd_ref, tile):
        return rr_ref[:, :1] / (dd_ref[:, :1] + unpack(tile, paths, 0, 1))

    def update_kernel(*refs):
        got = refs[:rows_n]
        d_ref, r_ref, rr_ref, dd_ref, out_ref, alpha_ref = refs[rows_n:]
        t = tree([g[...] for g in got])
        alpha = alpha_of(rr_ref, dd_ref, t[top:])
        mine = span(lax.axis_index("rows"), fc)
        image = d_ref[:, mine] + get_blocks(t, paths, fc)
        out_ref[...] = r_ref[:, mine] - alpha * image
        alpha_ref[...] = wide(alpha)

    def accumulate_kernel(alpha_ref, d_ref, ad_ref, x_ref, ax_ref, x_out, ax_out):
        alpha = alpha_ref[:, :1]
        x_out[...] = x_ref[...] + alpha * d_ref[...]
        ax_out[...] = ax_ref[...] + alpha * ad_ref[...]

    def start_kernel(*refs):
        got = refs[:rows_n]
        w_ref, p_ref, x_ref, out_ref = refs[rows_n:]
        mine = span(lax.axis_index("rows"), fc)
        t = get_blocks(tree([g[...] for g in got]), paths, fc)
        out_ref[...] = (w_ref[:, mine] - p_ref[:, mine] - x_ref[:, mine]) + t

    def begin_kernel(own, got, z_ref, u_ref, h_ref, l_ref, ax_ref, v_ref, *outs):
        core = core_half()
        ax_ref[:, span(core, half)] = get_blocks(own[...], paths, half)
        ax_ref[:, span(1 - core, half)] = get_blocks(got[...], paths, half)
        v = z_ref[...] - u_ref[...] - ax_ref[...]
        v_ref[...] = v
        whole_pieces(ahead, v, h_ref, l_ref, outs)

    def finish_kernel(final, *refs):
        sqs = refs[:rows_n]
        rr, dd, d, ad, x, ax, u, p, sign, lam = refs[rows_n : rows_n + 10]
        refs = refs[rows_n + 10 :]
        if not final:
            h_ref, l_ref = refs[:2]
            refs = refs[2:]
        x_out, ax_out, z_out, u_out, w_out, p_out = refs[:6]
        alpha = alpha_of(rr, dd, tree([s[...] for s in sqs]))
        x_new = x[...] + alpha * d[...]
        x_out[...] = x_new
        ax_out[...] = ax[...] + alpha * ad[...]

        @pl.loop(0, ns // tile)
        def _(j):
            cols = span(j, tile)
            target = ax_out[:, cols] + u[:, cols]
            m = prox(target, jnp.broadcast_to(sign[:1, cols], target.shape))
            z_out[:, cols] = m
            u_out[:, cols] = target - m

        total = x_new + p[...]
        mag = jnp.maximum(jnp.abs(total) - lam[:, :1], 0.0)
        w = jnp.where(total > 0.0, mag, jnp.where(total < 0.0, -mag, 0.0))
        w_out[...] = w
        p_out[...] = total - w
        if not final:
            v = z_out[...] - u_out[...] - ax_out[...]
            refs[6][...] = v
            whole_pieces(ahead, v, h_ref, l_ref, refs[7:])

    sign = jnp.broadcast_to((2.0 * labels.astype(f32) - 1.0)[None, :], (SUBLANES, ns))
    lam = jnp.broadcast_to(lambdas[:, None], one)

    x, w, p, z, u = x_prev, w_prev, p_prev, z_prev, u_prev
    hi, lo, t_hi, t_lo, blocks = prep(matrix, x)
    own, got = sum_cols(blocks[mid:], blocks[:mid])
    n_ahead, n_behind = [piece] * len(ahead), [piece] * len(behind)
    ax, v, *out = call(
        begin_kernel, [full_s, full_s] + n_ahead, (own, got, z, u, hi, lo), 2, work // 2
    )
    for outer in range(ITERS):
        sent = dict(zip(ahead, out))
        out = call(whole_behind_kernel, n_behind, (v, hi, lo), 2, work // 2)
        sent.update(zip(behind, out))
        pieces = {0: sent[0], **send_rows(sent)}
        pieces = [pieces[k] for k in range(rows_n)]
        (r_chunk,) = call(start_kernel, [chunk], (*pieces, w, p, x))
        for step in range(CG_STEPS):
            first = step == 0
            got = {0: r_chunk, **send_rows({k: r_chunk for k in order})}
            if not first:
                x, ax = call(accumulate_kernel, [full_f, full_s], (alpha, d, ad, x, ax))
            (acc,) = call(
                fwd_early_kernel, [full_s], (*[got[k] for k in early], t_hi, t_lo), 2,
                work // 2,
            )
            extra = () if first else (d,)
            other, r, scalars = call(
                functools.partial(fwd_other_kernel, first),
                [split, full_f, scal],
                (*[got[k] for k in early + late], *extra, acc, t_hi, t_lo),
                2,
                work // 4,
            )
            (own,) = call(
                fwd_own_kernel,
                [split],
                (*[got[k] for k in late], scalars, acc, t_hi, t_lo),
                2,
                work // 4,
            )
            own, got = sum_cols(other, own)
            olds = () if first else (ad, d, rr, dd)
            some = () if first else (ad, rr)
            outs = [(paths, half), full_f, one, one]
            if step + 1 < CG_STEPS:
                ad_own, d, rr, dd, acc = call(
                    functools.partial(bwd_own_kernel, first),
                    outs + [full_f],
                    (own, r, *olds, hi, lo),
                    2,
                    work // 2,
                )
                ad, scalars, *out = call(
                    functools.partial(bwd_ahead_kernel, first),
                    [full_s, scal] + n_ahead,
                    (got, ad_own, rr, *some, acc, hi, lo),
                    2,
                    work // 4,
                )
                sent = dict(zip(ahead, out))
                out = call(bwd_behind_kernel, n_behind, (ad, scalars, acc, hi, lo), 2, work // 4)
                sent.update(zip(behind, out))
                pieces = {0: sent[0], **send_rows(sent)}
                pieces = [pieces[k] for k in range(rows_n)]
                r_chunk, alpha = call(update_kernel, [chunk, one], (*pieces, d, r, rr, dd))
            else:
                ad_own, d, rr, dd = call(
                    lambda *refs: bwd_own_kernel(False, *refs[:6], None, None, *refs[6:], None),
                    outs,
                    (own, r, *olds),
                )
                ad, sq = call(last_kernel, [full_s, scal], (got, ad_own, rr, *some))
                sqs = {0: sq, **send_rows({k: sq for k in order})}
        ins = (*[sqs[k] for k in range(rows_n)], rr, dd, d, ad, x, ax, u, p, sign, lam)
        outs = [full_f, full_s, full_s, full_s, full_f, full_f]
        if outer + 1 < ITERS:
            x, ax, z, u, w, p, v, *out = call(
                functools.partial(finish_kernel, False),
                outs + [full_s] + n_ahead,
                (*ins, hi, lo),
                2,
                work // 2,
            )
        else:
            x, ax, z, u, w, p = call(functools.partial(finish_kernel, True), outs, ins)
    return x, w, z, u


def solution(mesh):
    return jax.shard_map(
        functools.partial(local, mesh.shape["rows"], mesh.shape["cols"]),
        mesh=mesh,
        in_specs=(
            P(("rep", "rows"), "cols"),
            P(("rep", "rows")),
            P("rep"),
            P("rep", "cols"),
            P("rep", "cols"),
            P("rep", "cols"),
            P("rep", "rows"),
            P("rep", "rows"),
        ),
        out_specs=(P("rep", "cols"), P("rep", "cols"), P("rep", "rows"), P("rep", "rows")),
        check_vma=False,
    )
```

time: 1310 us -> 356 us (0.27)
  waiting for transfers between devices: 614 us -> 146 us
  matrix products: 412 us -> 0 us
  blocking collectives: 230 us -> 0 us
  starting transfers between devices: 1.55 us -> 110 us
  Pallas kernels: 0 us -> 97.3 us
  other arithmetic: 25.7 us -> 0.39 us
  between operations: 14.8 us -> 1.17 us
    psum x23 -> x0, waiting for transfers between devices: 613 us -> none  [the longest x10 260 us: forward_with_norm(): lax.psum((apply_rows(vec, matrix), jnp.sum(vec * vec, axis=1)), 'cols')]
    dot_general x23 -> x0, matrix products: 412 us -> none  [the longest x13 253 us: apply_rows(): lax.dot_general(vec, matrix, (((1,), (1,)), ((), ())), precision=HIGH, pr...]
    psum x28 -> x0, blocking collectives: 230 us -> none  [the longest x10 118 us: cg_image(): back, sq_total = lax.psum((apply_cols(mapped, matrix), sq_part), 'rows')]
    ppermute x0 -> x99, waiting for transfers between devices: none -> 146 us  [xor_perm(): return lax.ppermute(x, axis, [(i, i ^ k) for i in range(size)])]
    ppermute x0 -> x99, starting transfers between devices: none -> 110 us  [xor_perm(): return lax.ppermute(x, axis, [(i, i ^ k) for i in range(size)])]
    pallas_call x0 -> x82, Pallas kernels: none -> 97.3 us  [the longest x81 85.9 us: call(): pl.pallas_call(body, in_specs=[VM] * len(args), out_specs=[VM] * len(outs...]
    reduce_sum x28 -> x0, other arithmetic: 16.9 us -> none  [the longest x10 11.9 us: squared_norm(): return lax.psum(jnp.sum(value * value, axis=1), 'cols')]
  transfers between devices with their start and end apart: 23 -> 99, of which waited for: 23 -> 80; matrix products, arithmetic and copies ran while one was open for 0% -> 0% of each run, Pallas kernels for 0% -> 13%
where the time goes in v1:
time: 356 us
  waiting for transfers between devices  146 us (41%)
  starting transfers between devices  110 us (31%)
  Pallas kernels  97.3 us (27%)
    ppermute x99, waiting for transfers between devices, xor_perm(): return lax.ppermute(x, axis, [(i, i ^ k) for i in range(size)])  146 us
    ppermute x99, starting transfers between devices, xor_perm(): return lax.ppermute(x, axis, [(i, i ^ k) for i in range(size)])  110 us
    pallas_call x81, Pallas kernels, call(): pl.pallas_call(body, in_specs=[VM] * len(args), out_specs=[VM] * len(outs...  85.9 us
    pallas_call x1, Pallas kernels, prep(): pl.pallas_call(prep_kernel, grid=(n // tile,), in_specs=[pl.BlockSpec((ti...  11.4 us
  transfers between devices with their start and end apart: 99, of which 80 were waited for; matrix products, arithmetic and copies ran while one was open for 0% of the time, Pallas kernels for 13%

profile of v1, /device:TPU:0, one launch (start us, length us, event | category | flops | bytes accessed | tf_op | source)
XLA Modules:
  0.0 355.9 jit_solution(15342554283680626021)
XLA Ops:
  1.6 11.4 %prep.1 = (bf16[2048,2048]{1,0:T(8,128)(2,1)S(1)}, bf16[2048,2048]{1,0:T(8,128)(2,1)S(1)}, bf16[2048,2048]{1,0:T(8,128)(2,1)S(1)}, bf16[2048,2048]{1,0:T(8,128)(2,1)S(1)}, f32[512,128]{1,0:T(8,128)S(1)}) custom-call(f32[2048,2048]{1,0:T(8,128)} %m_ref.1, f32[32,2048]{1,0:T(8,128)S(1)} %copy-done), custom_call_target="tpu_custom_call" | custom-call | tf_op jit(solution)/shard_map/prep/pallas_call | solution.py:142
  14.6 2.9 collective-permute-start.1
  17.5 3.8 %collective-permute-done.1 = f32[256,128]{1,0:T(8,128)S(1)} collective-permute-done((f32[256,128]{1,0:T(8,128)S(1)}, f32[256,128]{1,0:T(8,128)S(1)}, u32[]{:S(2)}, u32[]{:S(2)}) %collective-permute-start.1) | collective-permute-done | bytes 131104 | tf_op jit(solution)/shard_map/ppermute | solution.py:113
  27.8 2.6 collective-permute-start.4
  30.4 5.2 %collective-permute-done.4.refs_2_ = f32[136,128]{1,0:T(8,128)S(1)} collective-permute-done((f32[136,128]{1,0:T(8,128)S(1)}, f32[136,128]{1,0:T(8,128)S(1)}, u32[]{:S(2)}, u32[]{:S(2)}) %collective-permute-start.4) | collective-permute-done | bytes 69664 | tf_op jit(solution)/shard_map/ppermute | solution.py:113
  37.9 2.4 collective-permute-start.7
  49.7 4.1 %collective-permute-done.10 = f32[264,128]{1,0:T(8,128)S(1)} collective-permute-done((f32[264,128]{1,0:T(8,128)S(1)}, f32[264,128]{1,0:T(8,128)S(1)}, u32[]{:S(2)}, u32[]{:S(2)}) %collective-permute-start.10) | collective-permute-done | bytes 135200 | tf_op jit(solution)/shard_map/ppermute | solution.py:113
  53.9 2.0 shard_map.117
  57.7 3.0 collective-permute-start.13
  63.4 2.5 collective-permute-done.13.refs_2_
  68.5 2.4 collective-permute-start.16
  73.2 2.0 collective-permute-done.16.refs_3_.refs_1_
  81.2 4.1 %collective-permute-done.19 = f32[264,128]{1,0:T(8,128)S(1)} collective-permute-done((f32[264,128]{1,0:T(8,128)S(1)}, f32[264,128]{1,0:T(8,128)S(1)}, u32[]{:S(2)}, u32[]{:S(2)}) %collective-permute-start.19) | collective-permute-done | bytes 135200 | tf_op jit(solution)/shard_map/ppermute | solution.py:113
  85.4 2.1 shard_map.124
  89.3 2.8 collective-permute-start.22
  95.0 3.4 collective-permute-done.22.refs_2_
  100.1 2.2 collective-permute-start.25
  104.7 1.9 collective-permute-done.25.refs_3_.refs_1_
  112.7 4.1 %collective-permute-done.28 = f32[264,128]{1,0:T(8,128)S(1)} collective-permute-done((f32[264,128]{1,0:T(8,128)S(1)}, f32[264,128]{1,0:T(8,128)S(1)}, u32[]{:S(2)}, u32[]{:S(2)}) %collective-permute-start.28) | collective-permute-done | bytes 135200 | tf_op jit(solution)/shard_map/ppermute | solution.py:113
  116.9 2.2 shard_map.131
  120.9 2.7 collective-permute-start.31
  126.5 3.4 collective-permute-done.31.refs_2_
  131.7 2.1 collective-permute-start.34
  136.3 1.9 collective-permute-done.34.refs_3_.refs_1_
  144.2 4.1 %collective-permute-done.37 = f32[264,128]{1,0:T(8,128)S(1)} collective-permute-done((f32[264,128]{1,0:T(8,128)S(1)}, f32[264,128]{1,0:T(8,128)S(1)}, u32[]{:S(2)}, u32[]{:S(2)}) %collective-permute-start.37) | collective-permute-done | bytes 135200 | tf_op jit(solution)/shard_map/ppermute | solution.py:113
  148.4 2.1 shard_map.138
  152.3 2.6 collective-permute-start.40
  158.0 3.4 collective-permute-done.40.refs_2_
  163.1 2.0 collective-permute-start.43
  175.6 4.1 %collective-permute-done.46 = f32[264,128]{1,0:T(8,128)S(1)} collective-permute-done((f32[264,128]{1,0:T(8,128)S(1)}, f32[264,128]{1,0:T(8,128)S(1)}, u32[]{:S(2)}, u32[]{:S(2)}) %collective-permute-start.46) | collective-permute-done | bytes 135200 | tf_op jit(solution)/shard_map/ppermute | solution.py:113
  181.3 2.0 collective-permute-start.50
  183.3 2.4 collective-permute-start.48
  187.9 4.1 %shard_map.151 = (f32[32,2048]{1,0:T(8,128)S(1)}, f32[32,2048]{1,0:T(8,128)S(1)}, f32[32,2048]{1,0:T(8,128)}, f32[32,2048]{1,0:T(8,128)S(1)}, f32[32,2048]{1,0:T...) custom-call(f32[8,128]{1,0:T(8,128)S(1)} %get-tuple-element.266.refs, ...), custom_call_target="tpu_custom_call" | custom-call | flops 536870912 | bytes 18481152 | tf_op jit(solution)/shard_map/pallas_call | solution.py:31
  196.0 2.0 collective-permute-start.53
  198.1 4.1 %collective-permute-done.52.refs_2_ = f32[136,128]{1,0:T(8,128)S(1)} collective-permute-done((f32[136,128]{1,0:T(8,128)S(1)}, f32[136,128]{1,0:T(8,128)S(1)}, u32[]{:S(2)}, u32[]{:S(2)}) %collective-permute-start.52) | collective-permute-done | bytes 69664 | tf_op jit(solution)/shard_map/ppermute | solution.py:113
  203.6 2.0 collective-permute-start.55
  215.1 4.1 %collective-permute-done.58 = f32[264,128]{1,0:T(8,128)S(1)} collective-permute-done((f32[264,128]{1,0:T(8,128)S(1)}, f32[264,128]{1,0:T(8,128)S(1)}, u32[]{:S(2)}, u32[]{:S(2)}) %collective-permute-start.58) | collective-permute-done | bytes 135200 | tf_op jit(solution)/shard_map/ppermute | solution.py:113
  219.3 2.2 shard_map.157
  223.2 2.6 collective-permute-start.61
  228.9 3.4 collective-permute-done.61.refs_2_
  234.0 2.0 collective-permute-start.64
  240.5 1.9 collective-permute-done.63.refs_2_.refs_0_
  246.5 4.1 %collective-permute-done.67 = f32[264,128]{1,0:T(8,128)S(1)} collective-permute-done((f32[264,128]{1,0:T(8,128)S(1)}, f32[264,128]{1,0:T(8,128)S(1)}, u32[]{:S(2)}, u32[]{:S(2)}) %collective-permute-start.67) | collective-permute-done | bytes 135200 | tf_op jit(solution)/shard_map/ppermute | solution.py:113
  250.7 2.1 shard_map.164
  254.6 2.5 collective-permute-start.70
  260.3 3.4 collective-permute-done.70.refs_2_
  265.4 2.0 collective-permute-start.73
  271.9 1.9 collective-permute-done.72.refs_2_.refs_0_
  277.9 4.1 %collective-permute-done.76 = f32[264,128]{1,0:T(8,128)S(1)} collective-permute-done((f32[264,128]{1,0:T(8,128)S(1)}, f32[264,128]{1,0:T(8,128)S(1)}, u32[]{:S(2)}, u32[]{:S(2)}) %collective-permute-start.76) | collective-permute-done | bytes 135200 | tf_op jit(solution)/shard_map/ppermute | solution.py:113
  282.1 2.1 shard_map.171
  286.0 2.5 collective-permute-start.79
  291.7 3.4 collective-permute-done.79.refs_2_
  296.8 2.0 collective-permute-start.82
  303.2 1.9 collective-permute-done.81.refs_2_.refs_0_
  309.2 4.1 %collective-permute-done.85 = f32[264,128]{1,0:T(8,128)S(1)} collective-permute-done((f32[264,128]{1,0:T(8,128)S(1)}, f32[264,128]{1,0:T(8,128)S(1)}, u32[]{:S(2)}, u32[]{:S(2)}) %collective-permute-start.85) | collective-permute-done | bytes 135200 | tf_op jit(solution)/shard_map/ppermute | solution.py:113
  313.5 2.1 shard_map.178
  317.4 2.5 collective-permute-start.88
  323.0 3.4 collective-permute-done.88.refs_2_
  328.2 2.0 collective-permute-start.91
  334.6 1.9 collective-permute-done.90.refs_2_.refs_0_
  340.6 4.1 %collective-permute-done.94 = f32[264,128]{1,0:T(8,128)S(1)} collective-permute-done((f32[264,128]{1,0:T(8,128)S(1)}, f32[264,128]{1,0:T(8,128)S(1)}, u32[]{:S(2)}, u32[]{:S(2)}) %collective-permute-start.94) | collective-permute-done | bytes 135200 | tf_op jit(solution)/shard_map/ppermute | solution.py:113
  346.4 2.0 collective-permute-start.98
  348.3 2.4 collective-permute-start.96
  352.9 3.1 shard_map.191
  (258 shorter events, 166.3 us)
Async XLA Ops:
  14.6 6.7 %collective-permute-start.1 = (f32[256,128]{1,0:T(8,128)S(1)}, f32[256,128]{1,0:T(8,128)S(1)}, u32[]{:S(2)}, u32[]{:S(2)}) collective-permute-start(f32[256,128]{1,0:T(8,128)S(1)} %slice_add_fusion), channel_id=1, source_target_pairs={{0,4},{2,6},{4,0},{6,2},{1,5},{3,7},{5,1},{7,3},{8,12},{10,14},{12... | collective-permute-start | bytes 393224 | tf_op jit(solution)/shard_map/ppermute | solution.py:113
  27.8 7.8 %collective-permute-start.4 = (f32[136,128]{1,0:T(8,128)S(1)}, f32[136,128]{1,0:T(8,128)S(1)}, u32[]{:S(2)}, u32[]{:S(2)}) collective-permute-start(f32[136,128]{1,0:T(8,128)S(1)} %get-tuple-element.197), channel_id=1, source_target_pairs={{0,16},{8,24},{16,0},{24,8},{1,17},{9,25},{17,1},{25,9},{2,18},{10... | collective-permute-start | bytes 208904 | tf_op jit(solution)/shard_map/ppermute | solution.py:113
  30.4 6.2 %collective-permute-start.5 = (f32[136,128]{1,0:T(8,128)S(1)}, f32[136,128]{1,0:T(8,128)S(1)}, u32[]{:S(2)}, u32[]{:S(2)}) collective-permute-start(f32[136,128]{1,0:T(8,128)S(1)} %get-tuple-element.198), channel_id=1, source_target_pairs={{0,24},{8,16},{16,8},{24,0},{1,25},{9,17},{17,9},{25,1},{2,26},{10... | collective-permute-start | bytes 208904 | tf_op jit(solution)/shard_map/ppermute | solution.py:113
  36.6 5.0 %collective-permute-start.8 = (f32[32,512]{1,0:T(8,128)S(1)}, f32[32,512]{1,0:T(8,128)S(1)}, u32[]{:S(2)}, u32[]{:S(2)}) collective-permute-start(f32[32,512]{1,0:T(8,128)S(1)} %shard_map.113.refs_0_), channel_id=1, source_target_pairs={{0,8},{8,0},{16,24},{24,16},{1,9},{9,1},{17,25},{25,17},{2,10},{10... | collective-permute-start | bytes 196616 | tf_op jit(solution)/shard_map/ppermute | solution.py:113
  37.9 6.2 %collective-permute-start.7 = (f32[32,512]{1,0:T(8,128)S(1)}, f32[32,512]{1,0:T(8,128)S(1)}, u32[]{:S(2)}, u32[]{:S(2)}) collective-permute-start(f32[32,512]{1,0:T(8,128)S(1)} %shard_map.113.refs_0_), channel_id=1, source_target_pairs={{0,24},{8,16},{16,8},{24,0},{1,25},{9,17},{17,9},{25,1},{2,26},{10... | collective-permute-start | bytes 196616 | tf_op jit(solution)/shard_map/ppermute | solution.py:113
  40.3 5.3 %collective-permute-start.6 = (f32[32,512]{1,0:T(8,128)S(1)}, f32[32,512]{1,0:T(8,128)S(1)}, u32[]{:S(2)}, u32[]{:S(2)}) collective-permute-start(f32[32,512]{1,0:T(8,128)S(1)} %shard_map.113.refs_0_), channel_id=1, source_target_pairs={{0,16},{8,24},{16,0},{24,8},{1,17},{9,25},{17,1},{25,9},{2,18},{10... | collective-permute-start | bytes 196616 | tf_op jit(solution)/shard_map/ppermute | solution.py:113
  48.1 5.7 %collective-permute-start.10 = (f32[264,128]{1,0:T(8,128)S(1)}, f32[264,128]{1,0:T(8,128)S(1)}, u32[]{:S(2)}, u32[]{:S(2)}) collective-permute-start(f32[264,128]{1,0:T(8,128)S(1)} %add.69), channel_id=1, source_target_pairs={{0,4},{2,6},{4,0},{6,2},{1,5},{3,7},{5,1},{7,3},{8,12},{10,14},{12... | collective-permute-start | bytes 405512 | tf_op jit(solution)/shard_map/ppermute | solution.py:113
  57.7 5.8 %collective-permute-start.12 = (f32[136,128]{1,0:T(8,128)S(1)}, f32[136,128]{1,0:T(8,128)S(1)}, u32[]{:S(2)}, u32[]{:S(2)}) collective-permute-start(f32[136,128]{1,0:T(8,128)S(1)} %get-tuple-element.210), channel_id=1, source_target_pairs={{0,8},{8,0},{16,24},{24,16},{1,9},{9,1},{17,25},{25,17},{2,10},{10... | collective-permute-start | bytes 208904 | tf_op jit(solution)/shard_map/ppermute | solution.py:113
  57.7 8.3 %collective-permute-start.13 = (f32[136,128]{1,0:T(8,128)S(1)}, f32[136,128]{1,0:T(8,128)S(1)}, u32[]{:S(2)}, u32[]{:S(2)}) collective-permute-start(f32[136,128]{1,0:T(8,128)S(1)} %get-tuple-element.211), channel_id=1, source_target_pairs={{0,16},{8,24},{16,0},{24,8},{1,17},{9,25},{17,1},{25,9},{2,18},{10... | collective-permute-start | bytes 208904 | tf_op jit(solution)/shard_map/ppermute | solution.py:113
  60.7 6.1 %collective-permute-start.14 = (f32[136,128]{1,0:T(8,128)S(1)}, f32[136,128]{1,0:T(8,128)S(1)}, u32[]{:S(2)}, u32[]{:S(2)}) collective-permute-start(f32[136,128]{1,0:T(8,128)S(1)} %get-tuple-element.212), channel_id=1, source_target_pairs={{0,24},{8,16},{16,8},{24,0},{1,25},{9,17},{17,9},{25,1},{2,26},{10... | collective-permute-start | bytes 208904 | tf_op jit(solution)/shard_map/ppermute | solution.py:113
  68.5 6.6 %collective-permute-start.16 = (f32[32,512]{1,0:T(8,128)S(1)}, f32[32,512]{1,0:T(8,128)S(1)}, u32[]{:S(2)}, u32[]{:S(2)}) collective-permute-start(f32[32,512]{1,0:T(8,128)S(1)} %get-tuple-element.215.refs_0_), channel_id=1, source_target_pairs={{0,24},{8,16},{16,8},{24,0},{1,25},{9,17},{17,9},{25,1},{2,26},{10... | collective-permute-start | bytes 196616 | tf_op jit(solution)/shard_map/ppermute | solution.py:113
  71.0 6.1 %collective-permute-start.15 = (f32[32,512]{1,0:T(8,128)S(1)}, f32[32,512]{1,0:T(8,128)S(1)}, u32[]{:S(2)}, u32[]{:S(2)}) collective-permute-start(f32[32,512]{1,0:T(8,128)S(1)} %get-tuple-element.215.refs_0_), channel_id=1, source_target_pairs={{0,16},{8,24},{16,0},{24,8},{1,17},{9,25},{17,1},{25,9},{2,18},{10... | collective-permute-start | bytes 196616 | tf_op jit(solution)/shard_map/ppermute | solution.py:113
  79.6 5.7 %collective-permute-start.19 = (f32[264,128]{1,0:T(8,128)S(1)}, f32[264,128]{1,0:T(8,128)S(1)}, u32[]{:S(2)}, u32[]{:S(2)}) collective-permute-start(f32[264,128]{1,0:T(8,128)S(1)} %add.71), channel_id=1, source_target_pairs={{0,4},{2,6},{4,0},{6,2},{1,5},{3,7},{5,1},{7,3},{8,12},{10,14},{12... | collective-permute-start | bytes 405512 | tf_op jit(solution)/shard_map/ppermute | solution.py:113
  89.3 5.7 %collective-permute-start.21 = (f32[136,128]{1,0:T(8,128)S(1)}, f32[136,128]{1,0:T(8,128)S(1)}, u32[]{:S(2)}, u32[]{:S(2)}) collective-permute-start(f32[136,128]{1,0:T(8,128)S(1)} %get-tuple-element.225), channel_id=1, source_target_pairs={{0,8},{8,0},{16,24},{24,16},{1,9},{9,1},{17,25},{25,17},{2,10},{10... | collective-permute-start | bytes 208904 | tf_op jit(solution)/shard_map/ppermute | solution.py:113
  89.3 9.0 %collective-permute-start.22 = (f32[136,128]{1,0:T(8,128)S(1)}, f32[136,128]{1,0:T(8,128)S(1)}, u32[]{:S(2)}, u32[]{:S(2)}) collective-permute-start(f32[136,128]{1,0:T(8,128)S(1)} %get-tuple-element.226), channel_id=1, source_target_pairs={{0,16},{8,24},{16,0},{24,8},{1,17},{9,25},{17,1},{25,9},{2,18},{10... | collective-permute-start | bytes 208904 | tf_op jit(solution)/shard_map/ppermute | solution.py:113
  92.1 6.3 %collective-permute-start.23 = (f32[136,128]{1,0:T(8,128)S(1)}, f32[136,128]{1,0:T(8,128)S(1)}, u32[]{:S(2)}, u32[]{:S(2)}) collective-permute-start(f32[136,128]{1,0:T(8,128)S(1)} %get-tuple-element.227), channel_id=1, source_target_pairs={{0,24},{8,16},{16,8},{24,0},{1,25},{9,17},{17,9},{25,1},{2,26},{10... | collective-permute-start | bytes 208904 | tf_op jit(solution)/shard_map/ppermute | solution.py:113
  100.1 6.6 %collective-permute-start.25 = (f32[32,512]{1,0:T(8,128)S(1)}, f32[32,512]{1,0:T(8,128)S(1)}, u32[]{:S(2)}, u32[]{:S(2)}) collective-permute-start(f32[32,512]{1,0:T(8,128)S(1)} %get-tuple-element.230.refs_0_), channel_id=1, source_target_pairs={{0,24},{8,16},{16,8},{24,0},{1,25},{9,17},{17,9},{25,1},{2,26},{10... | collective-permute-start | bytes 196616 | tf_op jit(solution)/shard_map/ppermute | solution.py:113
  102.3 6.3 %collective-permute-start.24 = (f32[32,512]{1,0:T(8,128)S(1)}, f32[32,512]{1,0:T(8,128)S(1)}, u32[]{:S(2)}, u32[]{:S(2)}) collective-permute-start(f32[32,512]{1,0:T(8,128)S(1)} %get-tuple-element.230.refs_0_), channel_id=1, source_target_pairs={{0,16},{8,24},{16,0},{24,8},{1,17},{9,25},{17,1},{25,9},{2,18},{10... | collective-permute-start | bytes 196616 | tf_op jit(solution)/shard_map/ppermute | solution.py:113
  111.1 5.7 %collective-permute-start.28 = (f32[264,128]{1,0:T(8,128)S(1)}, f32[264,128]{1,0:T(8,128)S(1)}, u32[]{:S(2)}, u32[]{:S(2)}) collective-permute-start(f32[264,128]{1,0:T(8,128)S(1)} %add.73), channel_id=1, source_target_pairs={{0,4},{2,6},{4,0},{6,2},{1,5},{3,7},{5,1},{7,3},{8,12},{10,14},{12... | collective-permute-start | bytes 405512 | tf_op jit(solution)/shard_map/ppermute | solution.py:113
  120.9 5.7 %collective-permute-start.30 = (f32[136,128]{1,0:T(8,128)S(1)}, f32[136,128]{1,0:T(8,128)S(1)}, u32[]{:S(2)}, u32[]{:S(2)}) collective-permute-start(f32[136,128]{1,0:T(8,128)S(1)} %get-tuple-element.240), channel_id=1, source_target_pairs={{0,8},{8,0},{16,24},{24,16},{1,9},{9,1},{17,25},{25,17},{2,10},{10... | collective-permute-start | bytes 208904 | tf_op jit(solution)/shard_map/ppermute | solution.py:113
  120.9 9.0 %collective-permute-start.31 = (f32[136,128]{1,0:T(8,128)S(1)}, f32[136,128]{1,0:T(8,128)S(1)}, u32[]{:S(2)}, u32[]{:S(2)}) collective-permute-start(f32[136,128]{1,0:T(8,128)S(1)} %get-tuple-element.241), channel_id=1, source_target_pairs={{0,16},{8,24},{16,0},{24,8},{1,17},{9,25},{17,1},{25,9},{2,18},{10... | collective-permute-start | bytes 208904 | tf_op jit(solution)/shard_map/ppermute | solution.py:113
  123.5 6.4 %collective-permute-start.32 = (f32[136,128]{1,0:T(8,128)S(1)}, f32[136,128]{1,0:T(8,128)S(1)}, u32[]{:S(2)}, u32[]{:S(2)}) collective-permute-start(f32[136,128]{1,0:T(8,128)S(1)} %get-tuple-element.242), channel_id=1, source_target_pairs={{0,24},{8,16},{16,8},{24,0},{1,25},{9,17},{17,9},{25,1},{2,26},{10... | collective-permute-start | bytes 208904 | tf_op jit(solution)/shard_map/ppermute | solution.py:113
  131.7 6.5 %collective-permute-start.34 = (f32[32,512]{1,0:T(8,128)S(1)}, f32[32,512]{1,0:T(8,128)S(1)}, u32[]{:S(2)}, u32[]{:S(2)}) collective-permute-start(f32[32,512]{1,0:T(8,128)S(1)} %get-tuple-element.245.refs_0_), channel_id=1, source_target_pairs={{0,24},{8,16},{16,8},{24,0},{1,25},{9,17},{17,9},{25,1},{2,26},{10... | collective-permute-start | bytes 196616 | tf_op jit(solution)/shard_map/ppermute | solution.py:113
  133.8 6.3 %collective-permute-start.33 = (f32[32,512]{1,0:T(8,128)S(1)}, f32[32,512]{1,0:T(8,128)S(1)}, u32[]{:S(2)}, u32[]{:S(2)}) collective-permute-start(f32[32,512]{1,0:T(8,128)S(1)} %get-tuple-element.245.refs_0_), channel_id=1, source_target_pairs={{0,16},{8,24},{16,0},{24,8},{1,17},{9,25},{17,1},{25,9},{2,18},{10... | collective-permute-start | bytes 196616 | tf_op jit(solution)/shard_map/ppermute | solution.py:113
  142.6 5.7 %collective-permute-start.37 = (f32[264,128]{1,0:T(8,128)S(1)}, f32[264,128]{1,0:T(8,128)S(1)}, u32[]{:S(2)}, u32[]{:S(2)}) collective-permute-start(f32[264,128]{1,0:T(8,128)S(1)} %add.75), channel_id=1, source_target_pairs={{0,4},{2,6},{4,0},{6,2},{1,5},{3,7},{5,1},{7,3},{8,12},{10,14},{12... | collective-permute-start | bytes 405512 | tf_op jit(solution)/shard_map/ppermute | solution.py:113
  152.3 5.7 %collective-permute-start.39 = (f32[136,128]{1,0:T(8,128)S(1)}, f32[136,128]{1,0:T(8,128)S(1)}, u32[]{:S(2)}, u32[]{:S(2)}) collective-permute-start(f32[136,128]{1,0:T(8,128)S(1)} %get-tuple-element.255), channel_id=1, source_target_pairs={{0,8},{8,0},{16,24},{24,16},{1,9},{9,1},{17,25},{25,17},{2,10},{10... | collective-permute-start | bytes 208904 | tf_op jit(solution)/shard_map/ppermute | solution.py:113
  152.3 9.0 %collective-permute-start.40 = (f32[136,128]{1,0:T(8,128)S(1)}, f32[136,128]{1,0:T(8,128)S(1)}, u32[]{:S(2)}, u32[]{:S(2)}) collective-permute-start(f32[136,128]{1,0:T(8,128)S(1)} %get-tuple-element.256), channel_id=1, source_target_pairs={{0,16},{8,24},{16,0},{24,8},{1,17},{9,25},{17,1},{25,9},{2,18},{10... | collective-permute-start | bytes 208904 | tf_op jit(solution)/shard_map/ppermute | solution.py:113
  154.9 6.4 %collective-permute-start.41 = (f32[136,128]{1,0:T(8,128)S(1)}, f32[136,128]{1,0:T(8,128)S(1)}, u32[]{:S(2)}, u32[]{:S(2)}) collective-permute-start(f32[136,128]{1,0:T(8,128)S(1)} %get-tuple-element.257), channel_id=1, source_target_pairs={{0,24},{8,16},{16,8},{24,0},{1,25},{9,17},{17,9},{25,1},{2,26},{10... | collective-permute-start | bytes 208904 | tf_op jit(solution)/shard_map/ppermute | solution.py:113
  163.1 6.5 %collective-permute-start.43 = (f32[32,512]{1,0:T(8,128)S(1)}, f32[32,512]{1,0:T(8,128)S(1)}, u32[]{:S(2)}, u32[]{:S(2)}) collective-permute-start(f32[32,512]{1,0:T(8,128)S(1)} %get-tuple-element.260.refs_0_), channel_id=1, source_target_pairs={{0,24},{8,16},{16,8},{24,0},{1,25},{9,17},{17,9},{25,1},{2,26},{10... | collective-permute-start | bytes 196616 | tf_op jit(solution)/shard_map/ppermute | solution.py:113
  165.2 6.3 %collective-permute-start.42 = (f32[32,512]{1,0:T(8,128)S(1)}, f32[32,512]{1,0:T(8,128)S(1)}, u32[]{:S(2)}, u32[]{:S(2)}) collective-permute-start(f32[32,512]{1,0:T(8,128)S(1)} %get-tuple-element.260.refs_0_), channel_id=1, source_target_pairs={{0,16},{8,24},{16,0},{24,8},{1,17},{9,25},{17,1},{25,9},{2,18},{10... | collective-permute-start | bytes 196616 | tf_op jit(solution)/shard_map/ppermute | solution.py:113
  174.0 5.7 %collective-permute-start.46 = (f32[264,128]{1,0:T(8,128)S(1)}, f32[264,128]{1,0:T(8,128)S(1)}, u32[]{:S(2)}, u32[]{:S(2)}) collective-permute-start(f32[264,128]{1,0:T(8,128)S(1)} %add.77), channel_id=1, source_target_pairs={{0,4},{2,6},{4,0},{6,2},{1,5},{3,7},{5,1},{7,3},{8,12},{10,14},{12... | collective-permute-start | bytes 405512 | tf_op jit(solution)/shard_map/ppermute | solution.py:113
  181.3 5.4 %collective-permute-start.50 = (f32[8,128]{1,0:T(8,128)S(1)}, f32[8,128]{1,0:T(8,128)S(1)}, u32[]{:S(2)}, u32[]{:S(2)}) collective-permute-start(f32[8,128]{1,0:T(8,128)S(1)} %get-tuple-element.266.refs_0_), channel_id=1, source_target_pairs={{0,24},{8,16},{16,8},{24,0},{1,25},{9,17},{17,9},{25,1},{2,26},{10... | collective-permute-start | bytes 12296 | tf_op jit(solution)/shard_map/ppermute | solution.py:113
  183.3 4.5 %collective-permute-start.49 = (f32[8,128]{1,0:T(8,128)S(1)}, f32[8,128]{1,0:T(8,128)S(1)}, u32[]{:S(2)}, u32[]{:S(2)}) collective-permute-start(f32[8,128]{1,0:T(8,128)S(1)} %get-tuple-element.266.refs_0_), channel_id=1, source_target_pairs={{0,16},{8,24},{16,0},{24,8},{1,17},{9,25},{17,1},{25,9},{2,18},{10... | collective-permute-start | bytes 12296 | tf_op jit(solution)/shard_map/ppermute | solution.py:113
  193.6 4.5 %collective-permute-start.51 = (f32[136,128]{1,0:T(8,128)S(1)}, f32[136,128]{1,0:T(8,128)S(1)}, u32[]{:S(2)}, u32[]{:S(2)}) collective-permute-start(f32[136,128]{1,0:T(8,128)S(1)} %get-tuple-element.285), channel_id=1, source_target_pairs={{0,8},{8,0},{16,24},{24,16},{1,9},{9,1},{17,25},{25,17},{2,10},{10... | collective-permute-start | bytes 208904 | tf_op jit(solution)/shard_map/ppermute | solution.py:113
  195.1 7.1 %collective-permute-start.52 = (f32[136,128]{1,0:T(8,128)S(1)}, f32[136,128]{1,0:T(8,128)S(1)}, u32[]{:S(2)}, u32[]{:S(2)}) collective-permute-start(f32[136,128]{1,0:T(8,128)S(1)} %get-tuple-element.286), channel_id=1, source_target_pairs={{0,16},{8,24},{16,0},{24,8},{1,17},{9,25},{17,1},{25,9},{2,18},{10... | collective-permute-start | bytes 208904 | tf_op jit(solution)/shard_map/ppermute | solution.py:113
  196.0 6.2 %collective-permute-start.53 = (f32[136,128]{1,0:T(8,128)S(1)}, f32[136,128]{1,0:T(8,128)S(1)}, u32[]{:S(2)}, u32[]{:S(2)}) collective-permute-start(f32[136,128]{1,0:T(8,128)S(1)} %get-tuple-element.287), channel_id=1, source_target_pairs={{0,24},{8,16},{16,8},{24,0},{1,25},{9,17},{17,9},{25,1},{2,26},{10... | collective-permute-start | bytes 208904 | tf_op jit(solution)/shard_map/ppermute | solution.py:113
  203.6 6.1 %collective-permute-start.55 = (f32[32,512]{1,0:T(8,128)S(1)}, f32[32,512]{1,0:T(8,128)S(1)}, u32[]{:S(2)}, u32[]{:S(2)}) collective-permute-start(f32[32,512]{1,0:T(8,128)S(1)} %shard_map.153.refs_0_), channel_id=1, source_target_pairs={{0,24},{8,16},{16,8},{24,0},{1,25},{9,17},{17,9},{25,1},{2,26},{10... | collective-permute-start | bytes 196616 | tf_op jit(solution)/shard_map/ppermute | solution.py:113
  205.6 5.5 %collective-permute-start.54 = (f32[32,512]{1,0:T(8,128)S(1)}, f32[32,512]{1,0:T(8,128)S(1)}, u32[]{:S(2)}, u32[]{:S(2)}) collective-permute-start(f32[32,512]{1,0:T(8,128)S(1)} %shard_map.153.refs_0_), channel_id=1, source_target_pairs={{0,16},{8,24},{16,0},{24,8},{1,17},{9,25},{17,1},{25,9},{2,18},{10... | collective-permute-start | bytes 196616 | tf_op jit(solution)/shard_map/ppermute | solution.py:113
  213.5 5.7 %collective-permute-start.58 = (f32[264,128]{1,0:T(8,128)S(1)}, f32[264,128]{1,0:T(8,128)S(1)}, u32[]{:S(2)}, u32[]{:S(2)}) collective-permute-start(f32[264,128]{1,0:T(8,128)S(1)} %add.79), channel_id=1, source_target_pairs={{0,4},{2,6},{4,0},{6,2},{1,5},{3,7},{5,1},{7,3},{8,12},{10,14},{12... | collective-permute-start | bytes 405512 | tf_op jit(solution)/shard_map/ppermute | solution.py:113
  223.2 5.7 %collective-permute-start.60 = (f32[136,128]{1,0:T(8,128)S(1)}, f32[136,128]{1,0:T(8,128)S(1)}, u32[]{:S(2)}, u32[]{:S(2)}) collective-permute-start(f32[136,128]{1,0:T(8,128)S(1)} %get-tuple-element.300), channel_id=1, source_target_pairs={{0,8},{8,0},{16,24},{24,16},{1,9},{9,1},{17,25},{25,17},{2,10},{10... | collective-permute-start | bytes 208904 | tf_op jit(solution)/shard_map/ppermute | solution.py:113
  223.2 9.0 %collective-permute-start.61 = (f32[136,128]{1,0:T(8,128)S(1)}, f32[136,128]{1,0:T(8,128)S(1)}, u32[]{:S(2)}, u32[]{:S(2)}) collective-permute-start(f32[136,128]{1,0:T(8,128)S(1)} %get-tuple-element.301), channel_id=1, source_target_pairs={{0,16},{8,24},{16,0},{24,8},{1,17},{9,25},{17,1},{25,9},{2,18},{10... | collective-permute-start | bytes 208904 | tf_op jit(solution)/shard_map/ppermute | solution.py:113
  225.8 6.5 %collective-permute-start.62 = (f32[136,128]{1,0:T(8,128)S(1)}, f32[136,128]{1,0:T(8,128)S(1)}, u32[]{:S(2)}, u32[]{:S(2)}) collective-permute-start(f32[136,128]{1,0:T(8,128)S(1)} %get-tuple-element.302), channel_id=1, source_target_pairs={{0,24},{8,16},{16,8},{24,0},{1,25},{9,17},{17,9},{25,1},{2,26},{10... | collective-permute-start | bytes 208904 | tf_op jit(solution)/shard_map/ppermute | solution.py:113
  234.0 6.4 %collective-permute-start.64 = (f32[32,512]{1,0:T(8,128)S(1)}, f32[32,512]{1,0:T(8,128)S(1)}, u32[]{:S(2)}, u32[]{:S(2)}) collective-permute-start(f32[32,512]{1,0:T(8,128)S(1)} %get-tuple-element.305.refs_0_), channel_id=1, source_target_pairs={{0,24},{8,16},{16,8},{24,0},{1,25},{9,17},{17,9},{25,1},{2,26},{10... | collective-permute-start | bytes 196616 | tf_op jit(solution)/shard_map/ppermute | solution.py:113
  236.0 6.4 %collective-permute-start.63 = (f32[32,512]{1,0:T(8,128)S(1)}, f32[32,512]{1,0:T(8,128)S(1)}, u32[]{:S(2)}, u32[]{:S(2)}) collective-permute-start(f32[32,512]{1,0:T(8,128)S(1)} %get-tuple-element.305.refs_0_), channel_id=1, source_target_pairs={{0,16},{8,24},{16,0},{24,8},{1,17},{9,25},{17,1},{25,9},{2,18},{10... | collective-permute-start | bytes 196616 | tf_op jit(solution)/shard_map/ppermute | solution.py:113
  244.9 5.7 %collective-permute-start.67 = (f32[264,128]{1,0:T(8,128)S(1)}, f32[264,128]{1,0:T(8,128)S(1)}, u32[]{:S(2)}, u32[]{:S(2)}) collective-permute-start(f32[264,128]{1,0:T(8,128)S(1)} %add.81), channel_id=1, source_target_pairs={{0,4},{2,6},{4,0},{6,2},{1,5},{3,7},{5,1},{7,3},{8,12},{10,14},{12... | collective-permute-start | bytes 405512 | tf_op jit(solution)/shard_map/ppermute | solution.py:113
  254.6 5.7 %collective-permute-start.69 = (f32[136,128]{1,0:T(8,128)S(1)}, f32[136,128]{1,0:T(8,128)S(1)}, u32[]{:S(2)}, u32[]{:S(2)}) collective-permute-start(f32[136,128]{1,0:T(8,128)S(1)} %get-tuple-element.315), channel_id=1, source_target_pairs={{0,8},{8,0},{16,24},{24,16},{1,9},{9,1},{17,25},{25,17},{2,10},{10... | collective-permute-start | bytes 208904 | tf_op jit(solution)/shard_map/ppermute | solution.py:113
  254.6 9.0 %collective-permute-start.70 = (f32[136,128]{1,0:T(8,128)S(1)}, f32[136,128]{1,0:T(8,128)S(1)}, u32[]{:S(2)}, u32[]{:S(2)}) collective-permute-start(f32[136,128]{1,0:T(8,128)S(1)} %get-tuple-element.316), channel_id=1, source_target_pairs={{0,16},{8,24},{16,0},{24,8},{1,17},{9,25},{17,1},{25,9},{2,18},{10... | collective-permute-start | bytes 208904 | tf_op jit(solution)/shard_map/ppermute | solution.py:113
  257.2 6.5 %collective-permute-start.71 = (f32[136,128]{1,0:T(8,128)S(1)}, f32[136,128]{1,0:T(8,128)S(1)}, u32[]{:S(2)}, u32[]{:S(2)}) collective-permute-start(f32[136,128]{1,0:T(8,128)S(1)} %get-tuple-element.317), channel_id=1, source_target_pairs={{0,24},{8,16},{16,8},{24,0},{1,25},{9,17},{17,9},{25,1},{2,26},{10... | collective-permute-start | bytes 208904 | tf_op jit(solution)/shard_map/ppermute | solution.py:113
  265.4 6.4 %collective-permute-start.73 = (f32[32,512]{1,0:T(8,128)S(1)}, f32[32,512]{1,0:T(8,128)S(1)}, u32[]{:S(2)}, u32[]{:S(2)}) collective-permute-start(f32[32,512]{1,0:T(8,128)S(1)} %get-tuple-element.320.refs_0_), channel_id=1, source_target_pairs={{0,24},{8,16},{16,8},{24,0},{1,25},{9,17},{17,9},{25,1},{2,26},{10... | collective-permute-start | bytes 196616 | tf_op jit(solution)/shard_map/ppermute | solution.py:113
  267.4 6.4 %collective-permute-start.72 = (f32[32,512]{1,0:T(8,128)S(1)}, f32[32,512]{1,0:T(8,128)S(1)}, u32[]{:S(2)}, u32[]{:S(2)}) collective-permute-start(f32[32,512]{1,0:T(8,128)S(1)} %get-tuple-element.320.refs_0_), channel_id=1, source_target_pairs={{0,16},{8,24},{16,0},{24,8},{1,17},{9,25},{17,1},{25,9},{2,18},{10... | collective-permute-start | bytes 196616 | tf_op jit(solution)/shard_map/ppermute | solution.py:113
  276.3 5.7 %collective-permute-start.76 = (f32[264,128]{1,0:T(8,128)S(1)}, f32[264,128]{1,0:T(8,128)S(1)}, u32[]{:S(2)}, u32[]{:S(2)}) collective-permute-start(f32[264,128]{1,0:T(8,128)S(1)} %add.83), channel_id=1, source_target_pairs={{0,4},{2,6},{4,0},{6,2},{1,5},{3,7},{5,1},{7,3},{8,12},{10,14},{12... | collective-permute-start | bytes 405512 | tf_op jit(solution)/shard_map/ppermute | solution.py:113
  286.0 5.7 %collective-permute-start.78 = (f32[136,128]{1,0:T(8,128)S(1)}, f32[136,128]{1,0:T(8,128)S(1)}, u32[]{:S(2)}, u32[]{:S(2)}) collective-permute-start(f32[136,128]{1,0:T(8,128)S(1)} %get-tuple-element.330), channel_id=1, source_target_pairs={{0,8},{8,0},{16,24},{24,16},{1,9},{9,1},{17,25},{25,17},{2,10},{10... | collective-permute-start | bytes 208904 | tf_op jit(solution)/shard_map/ppermute | solution.py:113
  286.0 9.0 %collective-permute-start.79 = (f32[136,128]{1,0:T(8,128)S(1)}, f32[136,128]{1,0:T(8,128)S(1)}, u32[]{:S(2)}, u32[]{:S(2)}) collective-permute-start(f32[136,128]{1,0:T(8,128)S(1)} %get-tuple-element.331), channel_id=1, source_target_pairs={{0,16},{8,24},{16,0},{24,8},{1,17},{9,25},{17,1},{25,9},{2,18},{10... | collective-permute-start | bytes 208904 | tf_op jit(solution)/shard_map/ppermute | solution.py:113
  288.5 6.5 %collective-permute-start.80 = (f32[136,128]{1,0:T(8,128)S(1)}, f32[136,128]{1,0:T(8,128)S(1)}, u32[]{:S(2)}, u32[]{:S(2)}) collective-permute-start(f32[136,128]{1,0:T(8,128)S(1)} %get-tuple-element.332), channel_id=1, source_target_pairs={{0,24},{8,16},{16,8},{24,0},{1,25},{9,17},{17,9},{25,1},{2,26},{10... | collective-permute-start | bytes 208904 | tf_op jit(solution)/shard_map/ppermute | solution.py:113
  296.8 6.4 %collective-permute-start.82 = (f32[32,512]{1,0:T(8,128)S(1)}, f32[32,512]{1,0:T(8,128)S(1)}, u32[]{:S(2)}, u32[]{:S(2)}) collective-permute-start(f32[32,512]{1,0:T(8,128)S(1)} %get-tuple-element.335.refs_0_), channel_id=1, source_target_pairs={{0,24},{8,16},{16,8},{24,0},{1,25},{9,17},{17,9},{25,1},{2,26},{10... | collective-permute-start | bytes 196616 | tf_op jit(solution)/shard_map/ppermute | solution.py:113
  298.8 6.4 %collective-permute-start.81 = (f32[32,512]{1,0:T(8,128)S(1)}, f32[32,512]{1,0:T(8,128)S(1)}, u32[]{:S(2)}, u32[]{:S(2)}) collective-permute-start(f32[32,512]{1,0:T(8,128)S(1)} %get-tuple-element.335.refs_0_), channel_id=1, source_target_pairs={{0,16},{8,24},{16,0},{24,8},{1,17},{9,25},{17,1},{25,9},{2,18},{10... | collective-permute-start | bytes 196616 | tf_op jit(solution)/shard_map/ppermute | solution.py:113
  307.7 5.7 %collective-permute-start.85 = (f32[264,128]{1,0:T(8,128)S(1)}, f32[264,128]{1,0:T(8,128)S(1)}, u32[]{:S(2)}, u32[]{:S(2)}) collective-permute-start(f32[264,128]{1,0:T(8,128)S(1)} %add.85), channel_id=1, source_target_pairs={{0,4},{2,6},{4,0},{6,2},{1,5},{3,7},{5,1},{7,3},{8,12},{10,14},{12... | collective-permute-start | bytes 405512 | tf_op jit(solution)/shard_map/ppermute | solution.py:113
  317.3 5.7 %collective-permute-start.87 = (f32[136,128]{1,0:T(8,128)S(1)}, f32[136,128]{1,0:T(8,128)S(1)}, u32[]{:S(2)}, u32[]{:S(2)}) collective-permute-start(f32[136,128]{1,0:T(8,128)S(1)} %get-tuple-element.345), channel_id=1, source_target_pairs={{0,8},{8,0},{16,24},{24,16},{1,9},{9,1},{17,25},{25,17},{2,10},{10... | collective-permute-start | bytes 208904 | tf_op jit(solution)/shard_map/ppermute | solution.py:113
  317.4 9.0 %collective-permute-start.88 = (f32[136,128]{1,0:T(8,128)S(1)}, f32[136,128]{1,0:T(8,128)S(1)}, u32[]{:S(2)}, u32[]{:S(2)}) collective-permute-start(f32[136,128]{1,0:T(8,128)S(1)} %get-tuple-element.346), channel_id=1, source_target_pairs={{0,16},{8,24},{16,0},{24,8},{1,17},{9,25},{17,1},{25,9},{2,18},{10... | collective-permute-start | bytes 208904 | tf_op jit(solution)/shard_map/ppermute | solution.py:113
  319.9 6.5 %collective-permute-start.89 = (f32[136,128]{1,0:T(8,128)S(1)}, f32[136,128]{1,0:T(8,128)S(1)}, u32[]{:S(2)}, u32[]{:S(2)}) collective-permute-start(f32[136,128]{1,0:T(8,128)S(1)} %get-tuple-element.347), channel_id=1, source_target_pairs={{0,24},{8,16},{16,8},{24,0},{1,25},{9,17},{17,9},{25,1},{2,26},{10... | collective-permute-start | bytes 208904 | tf_op jit(solution)/shard_map/ppermute | solution.py:113
  328.2 6.4 %collective-permute-start.91 = (f32[32,512]{1,0:T(8,128)S(1)}, f32[32,512]{1,0:T(8,128)S(1)}, u32[]{:S(2)}, u32[]{:S(2)}) collective-permute-start(f32[32,512]{1,0:T(8,128)S(1)} %get-tuple-element.350.refs_0_), channel_id=1, source_target_pairs={{0,24},{8,16},{16,8},{24,0},{1,25},{9,17},{17,9},{25,1},{2,26},{10... | collective-permute-start | bytes 196616 | tf_op jit(solution)/shard_map/ppermute | solution.py:113
  330.2 6.4 %collective-permute-start.90 = (f32[32,512]{1,0:T(8,128)S(1)}, f32[32,512]{1,0:T(8,128)S(1)}, u32[]{:S(2)}, u32[]{:S(2)}) collective-permute-start(f32[32,512]{1,0:T(8,128)S(1)} %get-tuple-element.350.refs_0_), channel_id=1, source_target_pairs={{0,16},{8,24},{16,0},{24,8},{1,17},{9,25},{17,1},{25,9},{2,18},{10... | collective-permute-start | bytes 196616 | tf_op jit(solution)/shard_map/ppermute | solution.py:113
  339.0 5.7 %collective-permute-start.94 = (f32[264,128]{1,0:T(8,128)S(1)}, f32[264,128]{1,0:T(8,128)S(1)}, u32[]{:S(2)}, u32[]{:S(2)}) collective-permute-start(f32[264,128]{1,0:T(8,128)S(1)} %add.87), channel_id=1, source_target_pairs={{0,4},{2,6},{4,0},{6,2},{1,5},{3,7},{5,1},{7,3},{8,12},{10,14},{12... | collective-permute-start | bytes 405512 | tf_op jit(solution)/shard_map/ppermute | solution.py:113
  346.4 5.4 %collective-permute-start.98 = (f32[8,128]{1,0:T(8,128)S(1)}, f32[8,128]{1,0:T(8,128)S(1)}, u32[]{:S(2)}, u32[]{:S(2)}) collective-permute-start(f32[8,128]{1,0:T(8,128)S(1)} %get-tuple-element.356.refs_0_), channel_id=1, source_target_pairs={{0,24},{8,16},{16,8},{24,0},{1,25},{9,17},{17,9},{25,1},{2,26},{10... | collective-permute-start | bytes 12296 | tf_op jit(solution)/shard_map/ppermute | solution.py:113
  (43 other events, 202.1 us)
